TPU v7x, 16 devices: a 4x2x1 block of a 4x4x8 slice. The times are simulated.
16 devices in a mesh: data: 2 (over y, z), dap: 8 (over x, core).
Axes of the slice: x: 4, y: 2, z: 1, core: 2. Of those that a mesh axis runs over, the one named last changes fastest.
The devices are a block of a 4x4x8 slice.
Arguments:
- z_one: bfloat16 [1536, 768, 128], P(('data', 'dap')), parts along dimension 0
- mask_one: int32 [1536, 768], P(('data', 'dap')), parts along dimension 0
- z_two: bfloat16 [1536, 768, 128], P(('data', 'dap')), parts along dimension 0
- mask_two: int32 [1536, 768], P(('data', 'dap')), parts along dimension 0
- norm_in: bfloat16 [2, 2, 128], replicated
- w_proj: bfloat16 [2, 128, 512], replicated
- w_gate: bfloat16 [2, 128, 128], replicated
- norm_mid: bfloat16 [2, 2, 128], replicated
- w_out: bfloat16 [2, 128, 128], replicated
Outputs:
- output 1: bfloat16 [1536, 768, 128], P(('data', 'dap')), parts along dimension 0
- output 2: bfloat16 [1536, 768, 128], P(('data', 'dap')), parts along dimension 0
There are 2 independent parts. A program takes and returns all parts, laid end to end along the dimension named above; an argument that names none is the same for every part.
All inputs are finite; a program needn't handle non-finite values.
Results may differ from a plain program's by a relative error of at most 0.00447492.
Values are sent between devices in bfloat16 or wider.
A program may use at most 768 MiB of HBM per device.

v0:
```python
import jax
import jax.numpy as jnp
from jax import lax
from jax.sharding import PartitionSpec as P


def layer_norm(vals, ln_gain, ln_shift, feature_axis):
    vals = vals.astype(jnp.float32)
    row_mean = jnp.mean(vals, axis=feature_axis, keepdims=True)
    centred = vals - row_mean
    row_var = jnp.mean(centred * centred, axis=feature_axis, keepdims=True)
    return centred * lax.rsqrt(row_var + 1e-5) * ln_gain.astype(jnp.float32) + ln_shift.astype(jnp.float32)


def project_rows(z_rows, mask_rows, norm_in, w_proj):
    pair_width = z_rows.shape[2]
    hidden = w_proj.shape[1] // 4
    x_norm = layer_norm(z_rows, norm_in[0], norm_in[1], -1).astype(jnp.bfloat16)
    w_split = w_proj.reshape(pair_width, 2, 2, hidden)
    projected = jnp.einsum("rnz,zsgc->sgcrn", x_norm, w_split, preferred_element_type=jnp.float32)
    keep_mask = mask_rows.astype(jnp.float32)
    sides = (keep_mask * jax.nn.sigmoid(projected[:, 1]) * projected[:, 0]).astype(jnp.bfloat16)
    return x_norm, sides


def finish_rows(z_rows, x_norm, t_rows, w_gate, norm_mid, w_out):
    t_norm = layer_norm(t_rows, norm_mid[0][:, None, None], norm_mid[1][:, None, None], 0).astype(jnp.bfloat16)
    update = jnp.einsum("crn,cz->rnz", t_norm, w_out, preferred_element_type=jnp.float32)
    gate_val = jax.nn.sigmoid(jnp.einsum("rnz,zy->rny", x_norm, w_gate, preferred_element_type=jnp.float32))
    return (z_rows.astype(jnp.float32) + gate_val * update).astype(jnp.bfloat16)


def tri_update(z_rows, mask_rows, norm_in, w_proj, w_gate, norm_mid, w_out, form):
    x_norm, sides = project_rows(z_rows, mask_rows, norm_in, w_proj)
    sides_chan = lax.all_to_all(sides, "dap", 1, 2, tiled=True)
    tri_prod = jnp.einsum(form, sides_chan[0], sides_chan[1], preferred_element_type=jnp.float32).astype(jnp.bfloat16)
    t_rows = lax.all_to_all(tri_prod, "dap", 1, 0, tiled=True)
    return finish_rows(z_rows, x_norm, t_rows, w_gate, norm_mid, w_out)


def solution(mesh):
    row_spec = P(("data", "dap"), None, None)
    mask_spec = P(("data", "dap"), None)
    replicated = P()

    def crop_update(z_rows, mask_rows, norm_in, w_proj, w_gate, norm_mid, w_out):
        z_mid = tri_update(z_rows, mask_rows, norm_in[0], w_proj[0], w_gate[0], norm_mid[0], w_out[0], "cik,cjk->cij")
        return tri_update(z_mid, mask_rows, norm_in[1], w_proj[1], w_gate[1], norm_mid[1], w_out[1], "cki,ckj->cij")

    def per_device(z_one, mask_one, z_two, mask_two, norm_in, w_proj, w_gate, norm_mid, w_out):
        return (crop_update(z_one, mask_one, norm_in, w_proj, w_gate, norm_mid, w_out),
                crop_update(z_two, mask_two, norm_in, w_proj, w_gate, norm_mid, w_out))

    return jax.shard_map(per_device, mesh=mesh,
                         in_specs=(row_spec, mask_spec, row_spec, mask_spec, replicated, replicated, replicated, replicated, replicated),
                         out_specs=(row_spec, row_spec), check_vma=False)
```

profile of v0, /device:TPU:112, one launch (start us, length us, event | category | flops | bytes accessed | tf_op | source)
XLA Modules:
  0.0 3338.8 jit_solution(11907065030846813933)
XLA Ops:
  43.2 57.1 %convolution_bitcast_fusion.3 = f32[2,2,128,96,768]{2,4,1,0,3:T(8,128)} fusion(bf16[128,2,2,128,1]{0,3,2,1,4:T(8,128)(2,1)S(1)} %bitcast.301, bf16[96,768,128]{1,2,0:T(8,128)(2,1)} %copy.153, f32[128]{0:T(128)S(1)} %get-tuple-element.29, f32[128]{0:T(128)S(1)} %get-tuple-element.30, f32[96,768]{1,0:T(8,128)S(1)} %add_rsqrt_fusion.7, ...), kind=kOutput, calls=%fused_computation.52 | convolution fusion | flops 9720299520 | bytes 170591232 | tf_op jit(solution)/shard_map/rnz,zsgc->sgcrn/dot_general | solution.py:20
  100.3 59.1 %fusion.22 = bf16[2,128,96,768]{1,3,0,2:T(8,128)(2,1)} fusion(f32[2,2,128,96,768]{2,4,1,0,3:T(8,128)} %convolution_bitcast_fusion.3, f32[96,768]{1,0:T(8,128)S(1)} %convert_element_type.206), kind=kLoop, calls=%fused_computation.29 | loop fusion | flops 113246208 | bytes 189038592 | tf_op jit(solution)/shard_map/convert_element_type | solution.py:22
  159.5 91.8 %copy.160 = bf16[2,128,96,768]{3,0,2,1:T(2,128)(2,1)} copy(bf16[2,128,96,768]{1,3,0,2:T(8,128)(2,1)} %fusion.22) | data formatting | bytes 75497472 | tf_op jit(solution)/shard_map/convert_element_type | solution.py:22
  300.3 57.1 %convolution_bitcast_fusion.1 = f32[2,2,128,96,768]{2,4,0,3,1:T(8,128)} fusion(bf16[128,2,2,128,1]{0,3,2,1,4:T(8,128)(2,1)S(1)} %bitcast.302, bf16[96,768,128]{1,2,0:T(8,128)(2,1)} %copy.185, f32[96,768]{1,0:T(8,128)S(1)} %add_rsqrt_fusion.3, f32[96,768]{1,0:T(8,128)S(1)} %broadcast_multiply_fusion.3, f32[128]{0:T(128)S(1)} %get-tuple-element.29, ...), kind=kOutput, calls=%fused_computation.50 | convolution fusion | flops 9720299520 | bytes 170591232 | tf_op jit(solution)/shard_map/rnz,zsgc->sgcrn/dot_general | solution.py:20
  357.4 59.1 %fusion.8 = bf16[2,128,96,768]{1,3,0,2:T(8,128)(2,1)} fusion(f32[2,2,128,96,768]{2,4,0,3,1:T(8,128)} %convolution_bitcast_fusion.1, f32[96,768]{1,0:T(8,128)S(1)} %convert_element_type.235), kind=kLoop, calls=%fused_computation.11 | loop fusion | flops 113246208 | bytes 189038592 | tf_op jit(solution)/shard_map/convert_element_type | solution.py:22
  416.5 92.0 %copy.190 = bf16[2,128,96,768]{3,0,2,1:T(2,128)(2,1)} copy(bf16[2,128,96,768]{1,3,0,2:T(8,128)(2,1)} %fusion.8) | data formatting | bytes 75497472 | tf_op jit(solution)/shard_map/convert_element_type | solution.py:22
  508.5 159.8 %all-to-all-done = bf16[2,128,96,768]{3,0,2,1:T(2,128)(2,1)} async-done(((bf16[2,128,96,768]{3,0,2,1:T(2,128)(2,1)}), bf16[2,128,96,768]{3,0,2,1:T(2,128)(2,1)}, u32[]{:S(2)}, u32[]{:S(2)}) %all-to-all-start) | async-done | bytes 37748768 | tf_op jit(solution)/shard_map/all_to_all | solution.py:35
  804.7 280.5 %all-to-all-done.4 = bf16[2,128,96,768]{3,0,2,1:T(2,128)(2,1)} async-done(((bf16[2,128,96,768]{3,0,2,1:T(2,128)(2,1)}), bf16[2,128,96,768]{3,0,2,1:T(2,128)(2,1)}, u32[]{:S(2)}, u32[]{:S(2)}) %all-to-all-start.4) | async-done | bytes 37748768 | tf_op jit(solution)/shard_map/all_to_all | solution.py:35
  1221.4 76.8 %all-to-all-done.1 = bf16[16,768,768]{2,0,1:T(8,128)(2,1)} async-done(((bf16[16,768,768]{2,0,1:T(8,128)(2,1)}), bf16[16,768,768]{2,0,1:T(8,128)(2,1)}, u32[]{:S(2)}, u32[]{:S(2)}) %all-to-all-start.1) | async-done | bytes 18874400 | tf_op jit(solution)/shard_map/all_to_all | solution.py:37
  1342.7 169.0 %all-to-all-done.5 = bf16[16,768,768]{2,0,1:T(8,128)(2,1)} async-done(((bf16[16,768,768]{2,0,1:T(8,128)(2,1)}), bf16[16,768,768]{2,0,1:T(8,128)(2,1)}, u32[]{:S(2)}, u32[]{:S(2)}) %all-to-all-start.5) | async-done | bytes 18874400 | tf_op jit(solution)/shard_map/all_to_all | solution.py:37
  1571.7 33.2 convert_reduce_fusion.2
  1613.6 57.2 %convolution_bitcast_fusion.2 = f32[2,2,128,96,768]{2,4,0,3,1:T(8,128)} fusion(bf16[128,2,2,128,1]{0,3,2,1,4:T(8,128)(2,1)S(1)} %bitcast.299, bf16[96,768,128]{1,2,0:T(8,128)(2,1)} %get-tuple-element.35, f32[128]{0:T(128)S(1)} %copy-done.37, f32[128]{0:T(128)S(1)} %copy-done.34, f32[96,768]{1,0:T(8,128)S(1)} %add_rsqrt_fusion.5, ...), kind=kOutput, calls=%fused_computation.51 | convolution fusion | flops 9720299520 | bytes 170591232 | tf_op jit(solution)/shard_map/rnz,zsgc->sgcrn/dot_general | solution.py:20
  1670.8 59.1 %fusion.15 = bf16[2,128,96,768]{1,3,0,2:T(8,128)(2,1)} fusion(f32[2,2,128,96,768]{2,4,0,3,1:T(8,128)} %convolution_bitcast_fusion.2, f32[96,768]{1,0:T(8,128)S(1)} %copy-done.19), kind=kLoop, calls=%fused_computation.20 | loop fusion | flops 113246208 | bytes 189038592 | tf_op jit(solution)/shard_map/convert_element_type | solution.py:22
  1729.9 91.8 %copy.173 = bf16[2,128,96,768]{3,0,2,1:T(2,128)(2,1)} copy(bf16[2,128,96,768]{1,3,0,2:T(8,128)(2,1)} %fusion.15) | data formatting | bytes 75497472 | tf_op jit(solution)/shard_map/convert_element_type | solution.py:22
  1867.5 33.6 %convert_reduce_fusion = (f32[96,768]{1,0:T(8,128)S(1)}, bf16[96,768,128]{1,2,0:T(8,128)(2,1)}) fusion(bf16[128,96,768]{2,0,1:T(8,128)(2,1)} %bitcast.290, bf16[2,128,128]{2,1,0:T(8,128)(2,1)S(1)} %copy-done.41, f32[96,768,128]{1,2,0:T(8,128)} %fusion.102, bf16[96,768,128]{1,2,0:T(8,128)(2,1)} %copy.185), kind=kOutput, calls=%fused_computation.39 | convolution fusion | flops 2500780032 | bytes 94699520 | tf_op jit(solution)/shard_map/crn,cz->rnz/dot_general | solution.py:28
  1909.9 57.1 %convolution_bitcast_fusion = f32[2,2,128,96,768]{2,4,0,3,1:T(8,128)} fusion(bf16[128,2,2,128,1]{0,3,2,1,4:T(8,128)(2,1)S(1)} %bitcast.300, bf16[96,768,128]{1,2,0:T(8,128)(2,1)} %get-tuple-element.33, f32[96,768]{1,0:T(8,128)S(1)} %add_rsqrt_fusion.1, f32[96,768]{1,0:T(8,128)S(1)} %broadcast_multiply_fusion.1, f32[128]{0:T(128)S(1)} %copy-done.38, ...), kind=kOutput, calls=%fused_computation.49 | convolution fusion | flops 9720299520 | bytes 170591232 | tf_op jit(solution)/shard_map/rnz,zsgc->sgcrn/dot_general | solution.py:20
  1967.0 59.1 %fusion.1 = bf16[2,128,96,768]{1,3,0,2:T(8,128)(2,1)} fusion(f32[2,2,128,96,768]{2,4,0,3,1:T(8,128)} %convolution_bitcast_fusion, f32[96,768]{1,0:T(8,128)S(1)} %copy-done.15), kind=kLoop, calls=%fused_computation.2 | loop fusion | flops 113246208 | bytes 189038592 | tf_op jit(solution)/shard_map/convert_element_type | solution.py:22
  2026.1 92.0 %copy.201 = bf16[2,128,96,768]{3,0,2,1:T(2,128)(2,1)} copy(bf16[2,128,96,768]{1,3,0,2:T(8,128)(2,1)} %fusion.1) | data formatting | bytes 75497472 | tf_op jit(solution)/shard_map/convert_element_type | solution.py:22
  2118.1 120.5 %all-to-all-done.2 = bf16[2,128,96,768]{3,0,2,1:T(2,128)(2,1)} async-done(((bf16[2,128,96,768]{3,0,2,1:T(2,128)(2,1)}), bf16[2,128,96,768]{3,0,2,1:T(2,128)(2,1)}, u32[]{:S(2)}, u32[]{:S(2)}) %all-to-all-start.2) | async-done | bytes 37748768 | tf_op jit(solution)/shard_map/all_to_all | solution.py:35
  2371.5 284.0 %all-to-all-done.6 = bf16[2,128,96,768]{3,0,2,1:T(2,128)(2,1)} async-done(((bf16[2,128,96,768]{3,0,2,1:T(2,128)(2,1)}), bf16[2,128,96,768]{3,0,2,1:T(2,128)(2,1)}, u32[]{:S(2)}, u32[]{:S(2)}) %all-to-all-start.6) | async-done | bytes 37748768 | tf_op jit(solution)/shard_map/all_to_all | solution.py:35
  2788.3 80.5 %all-to-all-done.3 = bf16[16,768,768]{2,0,1:T(8,128)(2,1)} async-done(((bf16[16,768,768]{2,0,1:T(8,128)(2,1)}), bf16[16,768,768]{2,0,1:T(8,128)(2,1)}, u32[]{:S(2)}, u32[]{:S(2)}) %all-to-all-start.3) | async-done | bytes 18874400 | tf_op jit(solution)/shard_map/all_to_all | solution.py:37
  2900.1 181.6 %all-to-all-done.7 = bf16[16,768,768]{2,0,1:T(8,128)(2,1)} async-done(((bf16[16,768,768]{2,0,1:T(8,128)(2,1)}), bf16[16,768,768]{2,0,1:T(8,128)(2,1)}, u32[]{:S(2)}, u32[]{:S(2)}) %all-to-all-start.7) | async-done | bytes 18874400 | tf_op jit(solution)/shard_map/all_to_all | solution.py:37
  3177.2 34.1 %fusion.56 = bf16[96,768,128]{1,2,0:T(8,128)(2,1)} fusion(bf16[96,768,128]{1,2,0:T(8,128)(2,1)} %get-tuple-element.33, f32[96,768,128]{1,2,0:T(8,128)} %fusion.93, bf16[2,128,128]{2,1,0:T(8,128)(2,1)S(1)} %copy-done.45, f32[96,768]{1,0:T(8,128)S(1)} %copy-done.21, f32[96,768]{1,0:T(8,128)S(1)} %copy-done.13, f32[128]{0:T(128)S(1)} %copy-done.39, ...), kind=kOutput, calls=%fused_computation.80 | convolution fusion | flops 2538602496 | bytes 94995456 | tf_op jit(solution)/shard_map/rnz,zy->rny/dot_general | solution.py:29
  3279.6 34.4 %fusion.54 = bf16[96,768,128]{1,2,0:T(8,128)(2,1)} fusion(bf16[96,768,128]{1,2,0:T(8,128)(2,1)} %get-tuple-element.35, f32[96,768,128]{1,2,0:T(8,128)} %fusion.95, bf16[2,128,128]{2,1,0:T(8,128)(2,1)S(1)} %copy-done.45, f32[128]{0:T(128)S(1)} %copy-done.39, f32[128]{0:T(128)S(1)} %copy-done.36, f32[96,768]{1,0:T(8,128)S(1)} %copy-done.17, ...), kind=kOutput, calls=%fused_computation.78 | convolution fusion | flops 2538602496 | bytes 94995456 | tf_op jit(solution)/shard_map/rnz,zy->rny/dot_general | solution.py:29
  (235 shorter events, 1016.3 us)
Async XLA Ops:
  33.1 67.3 %copy-start.4 = (f32[96,768]{1,0:T(8,128)}, f32[96,768]{1,0:T(8,128)S(1)}, u32[]{:S(2)}) copy-start(f32[96,768]{1,0:T(8,128)S(1)} %broadcast_multiply_fusion.7) | copy-start | bytes 884740
  42.4 257.9 %copy-start.28 = (f32[128]{0:T(128)}, f32[128]{0:T(128)S(1)}, u32[]{:S(2)}) copy-start(f32[128]{0:T(128)S(1)} %get-tuple-element.29) | copy-start | bytes 1540
  42.4 257.9 %copy-start.31 = (f32[128]{0:T(128)}, f32[128]{0:T(128)S(1)}, u32[]{:S(2)}) copy-start(f32[128]{0:T(128)S(1)} %get-tuple-element.30) | copy-start | bytes 1540
  251.3 417.0 %all-to-all-start = ((bf16[2,128,96,768]{3,0,2,1:T(2,128)(2,1)}), bf16[2,128,96,768]{3,0,2,1:T(2,128)(2,1)}, u32[]{:S(2)}, u32[]{:S(2)}) async-start(bf16[2,128,96,768]{3,0,2,1:T(2,128)(2,1)} %copy.160), calls=%async_computation | async-start | bytes 75497472 | tf_op jit(solution)/shard_map/all_to_all | solution.py:35
  283.8 73.6 %copy-start.14 = (f32[96,768]{1,0:T(8,128)}, f32[96,768]{1,0:T(8,128)S(1)}, u32[]{:S(2)}) copy-start(f32[96,768]{1,0:T(8,128)S(1)} %convert_element_type.235) | copy-start | bytes 884740
  668.3 416.9 %all-to-all-start.4 = ((bf16[2,128,96,768]{3,0,2,1:T(2,128)(2,1)}), bf16[2,128,96,768]{3,0,2,1:T(2,128)(2,1)}, u32[]{:S(2)}, u32[]{:S(2)}) async-start(bf16[2,128,96,768]{3,0,2,1:T(2,128)(2,1)} %copy.190), calls=%async_computation.4 | async-start | bytes 75497472 | tf_op jit(solution)/shard_map/all_to_all | solution.py:35
  1085.2 213.1 %all-to-all-start.1 = ((bf16[16,768,768]{2,0,1:T(8,128)(2,1)}), bf16[16,768,768]{2,0,1:T(8,128)(2,1)}, u32[]{:S(2)}, u32[]{:S(2)}) async-start(bf16[16,768,768]{2,0,1:T(8,128)(2,1)} %copy.164), calls=%async_computation.1 | async-start | bytes 37748736 | tf_op jit(solution)/shard_map/all_to_all | solution.py:37
  1201.3 103.6 %copy-start.47 = (bf16[2,2,128]{2,1,0:T(2,128)(2,1)S(1)}, bf16[2,2,128]{2,1,0:T(2,128)(2,1)}, u32[]{:S(2)}) copy-start(bf16[2,2,128]{2,1,0:T(2,128)(2,1)} %param.16) | copy-start | bytes 3076
  1201.3 104.4 %copy-start.24 = (bf16[1,128,512]{2,1,0:T(8,128)(2,1)S(1)}, bf16[1,128,512]{2,1,0:T(8,128)(2,1)}, u32[]{:S(2)}) copy-start(bf16[1,128,512]{2,1,0:T(8,128)(2,1)} %get-tuple-element.22) | copy-start | bytes 393220
  1201.3 104.5 %copy-start.5 = (f32[96,768]{1,0:T(8,128)S(1)}, f32[96,768]{1,0:T(8,128)}, u32[]{:S(2)}) copy-start(f32[96,768]{1,0:T(8,128)} %copy-done.4) | copy-start | bytes 884740
  1201.3 104.5 %copy-start.9 = (f32[96,768]{1,0:T(8,128)S(1)}, f32[96,768]{1,0:T(8,128)}, u32[]{:S(2)}) copy-start(f32[96,768]{1,0:T(8,128)} %copy-done.8) | copy-start | bytes 884740
  1201.3 104.5 %copy-start.29 = (f32[128]{0:T(128)S(1)}, f32[128]{0:T(128)}, u32[]{:S(2)}) copy-start(f32[128]{0:T(128)} %copy-done.28) | copy-start | bytes 1540
  1201.3 104.5 %copy-start.32 = (f32[128]{0:T(128)S(1)}, f32[128]{0:T(128)}, u32[]{:S(2)}) copy-start(f32[128]{0:T(128)} %copy-done.31) | copy-start | bytes 1540
  1201.3 104.5 %copy-start.43 = (bf16[2,128,128]{2,1,0:T(8,128)(2,1)S(1)}, bf16[2,128,128]{2,1,0:T(8,128)(2,1)}, u32[]{:S(2)}) copy-start(bf16[2,128,128]{2,1,0:T(8,128)(2,1)} %param.15) | copy-start | bytes 196612
  1298.3 213.4 %all-to-all-start.5 = ((bf16[16,768,768]{2,0,1:T(8,128)(2,1)}), bf16[16,768,768]{2,0,1:T(8,128)(2,1)}, u32[]{:S(2)}, u32[]{:S(2)}) async-start(bf16[16,768,768]{2,0,1:T(8,128)(2,1)} %copy.194), calls=%async_computation.5 | async-start | bytes 37748736 | tf_op jit(solution)/shard_map/all_to_all | solution.py:37
  1305.8 307.8 %copy-start.22 = (bf16[1,128,512]{1,2,0:T(8,128)(2,1)}, bf16[1,128,512]{1,2,0:T(8,128)(2,1)S(1)}, u32[]{:S(2)}) copy-start(bf16[1,128,512]{1,2,0:T(8,128)(2,1)S(1)} %copy.253) | copy-start | bytes 393220
  1604.9 65.9 %copy-start.10 = (f32[96,768]{1,0:T(8,128)}, f32[96,768]{1,0:T(8,128)S(1)}, u32[]{:S(2)}) copy-start(f32[96,768]{1,0:T(8,128)S(1)} %broadcast_multiply_fusion.5) | copy-start | bytes 884740
  1821.8 416.8 %all-to-all-start.2 = ((bf16[2,128,96,768]{3,0,2,1:T(2,128)(2,1)}), bf16[2,128,96,768]{3,0,2,1:T(2,128)(2,1)}, u32[]{:S(2)}, u32[]{:S(2)}) async-start(bf16[2,128,96,768]{3,0,2,1:T(2,128)(2,1)} %copy.173), calls=%async_computation.2 | async-start | bytes 75497472 | tf_op jit(solution)/shard_map/all_to_all | solution.py:35
  1901.2 65.8 %copy-start.12 = (f32[96,768]{1,0:T(8,128)}, f32[96,768]{1,0:T(8,128)S(1)}, u32[]{:S(2)}) copy-start(f32[96,768]{1,0:T(8,128)S(1)} %broadcast_multiply_fusion.1) | copy-start | bytes 884740
  2238.6 416.9 %all-to-all-start.6 = ((bf16[2,128,96,768]{3,0,2,1:T(2,128)(2,1)}), bf16[2,128,96,768]{3,0,2,1:T(2,128)(2,1)}, u32[]{:S(2)}, u32[]{:S(2)}) async-start(bf16[2,128,96,768]{3,0,2,1:T(2,128)(2,1)} %copy.201), calls=%async_computation.6 | async-start | bytes 75497472 | tf_op jit(solution)/shard_map/all_to_all | solution.py:35
  2655.5 213.2 %all-to-all-start.3 = ((bf16[16,768,768]{2,0,1:T(8,128)(2,1)}), bf16[16,768,768]{2,0,1:T(8,128)(2,1)}, u32[]{:S(2)}, u32[]{:S(2)}) async-start(bf16[16,768,768]{2,0,1:T(8,128)(2,1)} %copy.178), calls=%async_computation.3 | async-start | bytes 37748736 | tf_op jit(solution)/shard_map/all_to_all | solution.py:37
  2768.2 106.7 %copy-start.49 = (f32[128]{0:T(128)S(1)}, f32[128]{0:T(128)}, u32[]{:S(2)}) copy-start(f32[128]{0:T(128)} %get-tuple-element.10) | copy-start | bytes 1540
  2768.2 106.9 %copy-start.48 = (f32[128]{0:T(128)S(1)}, f32[128]{0:T(128)}, u32[]{:S(2)}) copy-start(f32[128]{0:T(128)} %get-tuple-element.13) | copy-start | bytes 1540
  2868.7 213.0 %all-to-all-start.7 = ((bf16[16,768,768]{2,0,1:T(8,128)(2,1)}), bf16[16,768,768]{2,0,1:T(8,128)(2,1)}, u32[]{:S(2)}, u32[]{:S(2)}) async-start(bf16[16,768,768]{2,0,1:T(8,128)(2,1)} %copy.206), calls=%async_computation.7 | async-start | bytes 37748736 | tf_op jit(solution)/shard_map/all_to_all | solution.py:37
  (54 other events, 1521.5 us)
where the time goes:
time: 3360 us; the launch traced here: 3340 us
  waiting for transfers between devices  1350 us (40%)
  local copies, waits for them, and re-layouts  961 us (29%)
  matrix products  575 us (17%)
  other arithmetic  391 us (12%)
  starting transfers between devices  57.1 us (2%)
    all_to_all x4, waiting for transfers between devices, tri_update(): sides_chan = lax.all_to_all(sides, 'dap', 1, 2, tiled=True)  845 us
    all_to_all x4, waiting for transfers between devices, tri_update(): t_rows = lax.all_to_all(tri_prod, 'dap', 1, 0, tiled=True)  508 us
    convert_element_type x4, local copies, waits for them, and re-layouts, project_rows(): (keep_mask * jax.nn.sigmoid(projected[:, 1]) * projected[:, 0]).astype(jn...  368 us
    convert_element_type x4, other arithmetic, project_rows(): (keep_mask * jax.nn.sigmoid(projected[:, 1]) * projected[:, 0]).astype(jn...  236 us
    dot_general x4, matrix products, project_rows(): jnp.einsum('rnz,zsgc->sgcrn', x_norm, w_split, preferred_element_type=jnp...  229 us
    slice x8, local copies, waits for them, and re-layouts, tri_update(): sides_chan[1]  130 us
    dot_general x4, matrix products, finish_rows(): jnp.einsum('crn,cz->rnz', t_norm, w_out, preferred_element_type=jnp.float32)  120 us
    dot_general x4, matrix products, tri_update(): jnp.einsum(form, sides_chan[0], sides_chan[1], preferred_element_type=jnp...  117 us
  transfers between devices with their start and end apart: 8, of which 8 were waited for; matrix products, arithmetic and copies ran while one was open for 33% of the time, Pallas kernels for 0%

commit v1 on v0

v1 whole, which is shorter than its diff:
```python
import functools

import jax
import jax.numpy as jnp
from jax import lax
from jax.experimental import pallas as pl
from jax.experimental.pallas import tpu as pltpu
from jax.sharding import PartitionSpec as P


F32 = jnp.float32
BF16 = jnp.bfloat16
LANES = 128
ROWS = 16
STRIDE = 20
PAD = 4
AHEAD = 2
EPS = 1e-5
NT = (((1,), (1,)), ((), ()))
TN = (((0,), (0,)), ((), ()))
VMEM_LIMIT = 62 * 2 ** 20
COST = 0.02


def lane_norm(z, gain, shift):
    mean = jnp.mean(z, axis=-1, keepdims=True)
    cent = z - mean
    var = jnp.mean(cent * cent, axis=-1, keepdims=True)
    return (cent * lax.rsqrt(var + EPS) * gain + shift).astype(BF16)


def project_kernel(parts, sides, *refs):
    z_refs, mask_refs = refs[:parts], refs[parts:2 * parts]
    norm_ref, w_ref = refs[2 * parts:2 * parts + 2]
    out_refs, stage, x_ref = refs[2 * parts + 2:-2], refs[-2], refs[-1]
    hidden = w_ref.shape[0] // (2 * sides)
    depth = out_refs[0].shape[2]
    slabs = depth // LANES

    def prepare(i, slot):
        z = jnp.concatenate([r[i] for r in z_refs], axis=0)
        x_ref[slot] = lane_norm(z.astype(F32), norm_ref[0:1, :], norm_ref[1:2, :])

    def row(i, slot):
        keep = jnp.concatenate([r[pl.ds(i, 1), :] for r in mask_refs], axis=1).astype(F32) * 0.5
        q = lax.dot_general(w_ref[...], x_ref[slot], NT, preferred_element_type=F32)
        for side in range(sides):
            base = 2 * hidden * side
            val = (keep * jnp.tanh(q[base + hidden:base + 2 * hidden]) + keep) * q[base:base + hidden]
            for slab in range(slabs):
                stage[side * slabs + slab, pl.ds(i, hidden, stride=STRIDE), :] = val[:, slab * LANES:(slab + 1) * LANES]

    ahead = AHEAD
    for k in range(ahead):
        prepare(k, k)

    def rows_step(g, carry):
        for k in range(ahead):
            row(g * ahead + k, k)
            prepare(jnp.minimum(g * ahead + k + ahead, ROWS - 1), k)
        return carry

    lax.fori_loop(0, ROWS // ahead, rows_step, 0)
    group = 16

    def flush(g, carry):
        for side in range(sides):
            for slab in range(slabs):
                for c in range(group):
                    vals = stage[side * slabs + slab, pl.ds((g * group + c) * STRIDE, ROWS), :].astype(BF16)
                    out_refs[side][g * group + c, :, slab * LANES:(slab + 1) * LANES] = vals
        return carry

    lax.fori_loop(0, hidden // group, flush, 0)


def project(z_parts, mask_parts, norm, w_t, sides):
    rows = z_parts[0].shape[0]
    depths = [z.shape[1] for z in z_parts]
    depth = sum(depths)
    width = z_parts[0].shape[2]
    w_t = w_t[w_t.shape[0] // 2 * (2 - sides):]
    hidden = w_t.shape[0] // (2 * sides)
    gates = jnp.arange(w_t.shape[0]) // hidden % 2 == 1
    w_t = jnp.where(gates[:, None], w_t * 0.5, w_t).astype(BF16)
    whole = lambda x: pl.BlockSpec(x.shape, lambda i: (0,) * x.ndim)
    return pl.pallas_call(
        functools.partial(project_kernel, len(z_parts), sides),
        grid=(rows // ROWS,),
        in_specs=[pl.BlockSpec((ROWS, d, width), lambda i: (i, 0, 0)) for d in depths]
        + [pl.BlockSpec((ROWS, d), lambda i: (i, 0)) for d in depths] + [whole(norm), whole(w_t)],
        out_specs=[pl.BlockSpec((hidden, ROWS, depth), lambda i: (0, i, 0))] * sides,
        out_shape=[jax.ShapeDtypeStruct((hidden, rows, depth), BF16)] * sides,
        scratch_shapes=[pltpu.VMEM((sides * depth // LANES, hidden * STRIDE, LANES), F32),
                        pltpu.VMEM((AHEAD, depth, width), BF16)],
        compiler_params=pltpu.CompilerParams(vmem_limit_bytes=VMEM_LIMIT),
        cost_estimate=pl.CostEstimate(flops=int(COST * 1e9 * (0.4 if sides == 1 else 0.5)), transcendentals=0,
                                      bytes_accessed=rows * depth * (2 * width + 2 * hidden * sides)),
        name="project",
    )(*z_parts, *mask_parts, norm, w_t)


def mix_kernel(pieces, half, n_in, info, *refs):
    a_refs, b_refs = refs[:pieces], refs[pieces:pieces + 2]
    z_ref, norm_ref, mid_ref, w_gate_ref, w_out_ref = refs[pieces + 2:pieces + 7]
    out_ref, acc = refs[n_in:]
    step = pl.program_id(0)
    chunk, rows, _ = a_refs[0].shape
    pitch = rows + PAD
    channels = acc.shape[1] // pitch

    for c in range(chunk):
        a = jnp.concatenate([r[c] for r in a_refs], axis=1) if pieces > 1 else a_refs[0][c]
        for h in range(2):
            if pieces > 1:
                b = jnp.concatenate([r[c, h * half:(h + 1) * half] for r in b_refs], axis=1)
            else:
                b = b_refs[h][c]
            t = lax.dot_general(a, b, NT, preferred_element_type=F32)
            acc[h, pl.ds((step * chunk + c) * pitch, rows), 0:half] = t.astype(BF16).astype(F32)

    @pl.when(step == pl.num_programs(0) - 1)
    def _():
        flip = info[2] if pieces == 1 else 0
        starts = [pl.multiple_of(flip * half, 32), pl.multiple_of((1 - flip) * half, 32)]

        def row(i, carry):
            t = jnp.concatenate([acc[h, pl.ds(i, channels, stride=pitch), :] for h in range(2)], axis=1)
            cent = t - jnp.mean(t, axis=0, keepdims=True)
            var = jnp.mean(cent * cent, axis=0, keepdims=True)
            y = (cent * lax.rsqrt(var + EPS) * mid_ref[0] + mid_ref[1]).astype(BF16)
            update = lax.dot_general(y, w_out_ref[...], TN, preferred_element_type=F32)
            z = jnp.concatenate([z_ref[i, pl.ds(s, half), :] for s in starts], axis=0).astype(F32)
            x = lane_norm(z, norm_ref[0:1, :], norm_ref[1:2, :])
            gate = 0.5 * jnp.tanh(0.5 * jnp.dot(x, w_gate_ref[...], preferred_element_type=F32)) + 0.5
            update = jnp.concatenate([update[0:half], update[LANES:LANES + half]], axis=0)
            new = (z + gate * update).astype(BF16)
            for h, s in enumerate(starts):
                out_ref[i, pl.ds(s, half), :] = new[h * half:(h + 1) * half]
            return carry

        lax.fori_loop(0, rows, row, 0, unroll=4)


def mix(a_parts, b_parts, z, col_block, core, norm, mid, w_gate, w_out, rows, whole=None, dest=None):
    pieces = len(a_parts)
    hidden, _, depth = a_parts[0].shape
    half = b_parts[0].shape[1] // (1 if pieces == 1 else 2)
    cols, width = 2 * half, z.shape[2]
    chunk = 8
    pick = (lambda c, s: (c, 0, 0)) if pieces == 1 else (lambda c, s: (c, s[2], 0))
    zero = jnp.zeros((), jnp.int32)
    info = jnp.stack([col_block, zero if dest is None else dest, core]).astype(jnp.int32)
    mid_wide = jnp.broadcast_to(mid[:, :, None], (*mid.shape, 2 * LANES))
    fixed = lambda x: pl.BlockSpec(x.shape, lambda c, s: (0,) * x.ndim)
    args = [*a_parts, *b_parts, z, norm, mid_wide, w_gate, w_out]
    in_specs = ([pl.BlockSpec((chunk, rows, depth), pick)] * pieces
                + [pl.BlockSpec((chunk, b_parts[0].shape[1], depth), lambda c, s: (c, 0, 0))] * 2
                + [pl.BlockSpec((rows, cols, width), lambda c, s: (0, s[0], 0))] + [fixed(x) for x in args[pieces + 3:]])
    alias = {}
    total = cols if whole is None else whole if isinstance(whole, int) else whole.shape[1]
    if total != cols and not isinstance(whole, int):
        alias = {1 + len(args): 0}
        args.append(whole)
        in_specs.append(pl.BlockSpec(memory_space=pl.ANY))
    return pl.pallas_call(
        functools.partial(mix_kernel, pieces, half, len(args)),
        grid_spec=pltpu.PrefetchScalarGridSpec(
            num_scalar_prefetch=1, grid=(hidden // chunk,), in_specs=in_specs,
            out_specs=pl.BlockSpec((rows, cols, width), lambda c, s: (0, s[1], 0)),
            scratch_shapes=[pltpu.VMEM((2, hidden * (rows + PAD), LANES), F32)]),
        out_shape=jax.ShapeDtypeStruct((rows, total, width), BF16),
        input_output_aliases=alias,
        compiler_params=pltpu.CompilerParams(vmem_limit_bytes=VMEM_LIMIT),
        cost_estimate=pl.CostEstimate(flops=int(COST * 0.45e9), transcendentals=0,
                                      bytes_accessed=2 * hidden * depth * pieces * (rows + cols)),
        name="mix",
    )(info, *args)


def solution(mesh):
    group = mesh.shape["dap"]
    cores = 2
    chips = group // cores

    def shift(x, by):
        return lax.ppermute(x, "dap", [(((c + by) % chips) * cores + s, c * cores + s) for c in range(chips) for s in range(cores)])

    def swap(x):
        return lax.ppermute(x, "dap", [(i, i ^ 1) for i in range(group)])

    def per_device(z_one, mask_one, z_two, mask_two, norm_in, w_proj, w_gate, norm_mid, w_out):
        assert chips == 4
        index = lax.axis_index("dap")
        chip, core = index // cores, index % cores
        hidden = w_out.shape[1]
        rows = z_one.shape[0]
        cols = rows * cores
        zero = jnp.zeros((), jnp.int32)
        turns = (1, -1)
        crops = range(len(turns))
        z0, mask = (z_one, z_two), (mask_one, mask_two)

        def weights(u):
            w = w_proj[u].reshape(w_proj.shape[1], 2, 2, hidden)
            w_t = w.transpose(1, 2, 3, 0).reshape(4 * hidden, -1)
            norm = norm_in[u].astype(F32)
            return (norm, w_t), (norm, norm_mid[u].astype(F32), w_gate[u], w_out[u], rows)

        def at(n, ahead):
            return (chip + turns[n] * ahead) % chips

        def mask_rows(n, ahead):
            return lax.dynamic_slice_in_dim(whole_mask[n], (at(n, ahead) * cores + core) * rows, rows, 0)

        def mask_cols(n, ahead):
            strip = lax.dynamic_slice_in_dim(mask_t[n], at(n, ahead) * cols, cols, 0)
            return [lax.dynamic_slice_in_dim(strip, (at(n, r) * cores + core) * rows, rows, 1) for r in range(chips)]

        turned = lambda x: jnp.swapaxes(x, 0, 1)
        tie = lax.optimization_barrier

        par, fin = weights(0)
        z1 = [shift(z0[n], turns[n]) for n in crops]
        whole_mask = [lax.all_gather(m, "dap", axis=0, tiled=True) for m in mask]
        ab0 = [project([z0[n]], [mask[n]], *par, 2) for n in crops]
        b0s = [swap(ab0[n][1]) for n in crops]
        x00 = [mix([ab0[n][0]], [ab0[n][1], b0s[n]], z0[n], at(n, 0), core, *fin) for n in crops]
        z1, x00, whole_mask = tie((z1, x00, whole_mask))
        z2 = [shift(z1[n], turns[n]) for n in crops]
        ab1 = [project([z1[n]], [mask_rows(n, 1)], *par, 2) for n in crops]
        b1s = [swap(ab1[n][1]) for n in crops]
        x10 = [mix([ab1[n][0]], [ab0[n][1], b0s[n]], z1[n], at(n, 0), core, *fin) for n in crops]
        x01 = [mix([ab0[n][0]], [ab1[n][1], b1s[n]], z0[n], at(n, 1), core, *fin) for n in crops]
        t00, t10, t01 = [[turned(x[n]) for n in crops] for x in (x00, x10, x01)]
        mask_t = [m.T for m in whole_mask]

        first, second = crops
        l1 = [shift(x[first], turns[first]) for x in (t00, t10, t01)]
        r1 = [shift(t01[first], -turns[first])]
        z2, t00, t10, t01 = tie((z2, t00, t10, t01))
        b2, b2s, x02, t02 = [None] * 2, [None] * 2, [None] * 2, [None] * 2
        for n in crops:
            b2[n], = project([z2[n]], [mask_rows(n, 2)], *par, 1)
            b2s[n] = swap(b2[n])
        x02[first] = mix([ab0[first][0]], [b2[first], b2s[first]], z0[first], at(first, 2), core, *fin)
        t02[first], b2[second] = tie((turned(x02[first]), b2[second]))
        r1.append(shift(t02[first], -turns[first]))
        x02[second] = mix([ab0[second][0]], [b2[second], b2s[second]], z0[second], at(second, 2), core, *fin)
        t02[second] = turned(x02[second])

        par, fin = weights(1)

        def columns(n, got):
            t11, t21, t12, t30, t31, t22, t32, t20 = got
            return ([t00[n], t10[n], t20, t30], [t01[n], t11, t21, t31], [t02[n], t12, t22, t32])

        def column(n, k, parts):
            return project(parts, mask_cols(n, k), *par, 1 if k == 2 else 2)

        def both(sides):
            return sides, [swap(s) for s in sides]

        def turn_block(one, two, x, **where):
            (own, other), (own_b, other_b) = one, two
            return mix([own[0], other[0]], [own_b[-1], other_b[-1]], x, zero, core, *fin, **where)

        l1, r1, own = tie((l1, r1, (t00[second], t10[second], t01[second], t02[second])))
        t00[second], t10[second], t01[second], t02[second] = own
        r2 = shift(r1[1], -turns[first])
        l2 = [shift(x, turns[first]) for x in l1[:2]]
        m1 = [shift(x[second], turns[second]) for x in (t00, t10, t01)]
        s1 = [shift(x[second], -turns[second]) for x in (t01, t02)]

        n = first
        col0, col1, col2 = columns(n, (*l1, *r1, *l2, r2))
        c1, col0 = tie((column(n, 1, col1), col0))
        c1 = both(c1)
        c0 = both(column(n, 0, col0))
        y10 = turn_block(c1, c0, x10[n])
        y03 = shift(y10, -turns[n])
        out, y10 = tie((x00[n], y10))
        out = turn_block(c0, c0, out, whole=cols * chips, dest=at(n, 0))
        out = turn_block(c0, c1, x01[n], whole=out, dest=at(n, 1))
        m1, col2, out = tie((m1, col2, out))
        m2 = [shift(x, turns[second]) for x in m1[:2]]
        c2 = both(column(n, 2, col2))
        out = turn_block(c0, c2, x02[n], whole=out, dest=at(n, 2))
        s1, out, m1 = tie((s1, out, m1))
        s2 = shift(s1[1], -turns[second])
        out_one = lax.dynamic_update_slice_in_dim(out, y03, at(n, 3) * cols, 1)

        n = second
        col0, col1, col2 = columns(n, (*m1, *s1, *m2, s2))
        c1, col0 = tie((column(n, 1, col1), col0))
        c1 = both(c1)
        c0, col2 = tie((column(n, 0, col0), col2))
        c0 = both(c0)
        c2, last = tie((column(n, 2, col2), x10[n]))
        c2 = both(c2)
        y10 = turn_block(c1, c0, last)
        y03 = shift(y10, -turns[n])
        out, y10 = tie((x00[n], y10))
        out = turn_block(c0, c0, out, whole=cols * chips, dest=at(n, 0))
        out = turn_block(c0, c1, x01[n], whole=out, dest=at(n, 1))
        out = turn_block(c0, c2, x02[n], whole=out, dest=at(n, 2))
        out_two = lax.dynamic_update_slice_in_dim(out, y03, at(n, 3) * cols, 1)
        return out_one, out_two


    row_spec = P(("data", "dap"), None, None)
    mask_spec = P(("data", "dap"), None)
    return jax.shard_map(per_device, mesh=mesh,
                         in_specs=(row_spec, mask_spec, row_spec, mask_spec, P(), P(), P(), P(), P()),
                         out_specs=(row_spec, row_spec), check_vma=False)
```

time: 3360 us -> 2710 us (0.81)
  Pallas kernels: 0 us -> 1300 us
  local copies, waits for them, and re-layouts: 961 us -> 83.6 us
  matrix products: 575 us -> 0 us
  other arithmetic: 391 us -> 9.64 us
  waiting for transfers between devices: 1350 us -> 1270 us
    all_to_all x8 -> x0, waiting for transfers between devices: 1350 us -> none  [the longest x4 845 us: tri_update(): sides_chan = lax.all_to_all(sides, 'dap', 1, 2, tiled=True)]
    pallas_call x0 -> x28, Pallas kernels: none -> 1300 us  [the longest x16 706 us: mix(): pl.pallas_call(functools.partial(mix_kernel, pieces, half, len(args)), gr...]
    ppermute x0 -> x38, waiting for transfers between devices: none -> 1270 us  [the longest x22 1130 us: shift(): lax.ppermute(x, 'dap', [((c + by) % chips * cores + s, c * cores + s) for...]
    dot_general x16 -> x0, matrix products: 575 us -> none  [the longest x4 229 us: project_rows(): jnp.einsum('rnz,zsgc->sgcrn', x_norm, w_split, preferred_element_type=jnp...]
    convert_element_type x18 -> x0, local copies, waits for them, and re-layouts: 518 us -> none  [the longest x4 368 us: project_rows(): (keep_mask * jax.nn.sigmoid(projected[:, 1]) * projected[:, 0]).astype(jn...]
    convert_element_type x9 -> x2, other arithmetic: 290 us -> 1.86 us  [the longest x1 1.27 us: weights(): norm = norm_in[u].astype(F32)]
    slice x13 -> x3, local copies, waits for them, and re-layouts: 210 us -> 1 us  [the longest x1 0.99 us: weights(): w = w_proj[u].reshape(w_proj.shape[1], 2, 2, hidden)]
    all_to_all x6 -> x0, local copies, waits for them, and re-layouts: 128 us -> none  [the longest x4 102 us: tri_update(): sides_chan = lax.all_to_all(sides, 'dap', 1, 2, tiled=True)]
  transfers between devices with their start and end apart: 8 -> 40, of which waited for: 8 -> 18; matrix products, arithmetic and copies ran while one was open for 33% -> 3% of each run, Pallas kernels for 0% -> 39%
where the time goes in v1:
time: 2710 us; the launch traced here: 2700 us
  Pallas kernels  1300 us (48%)
  waiting for transfers between devices  1270 us (47%)
  local copies, waits for them, and re-layouts  83.6 us (3%)
    ppermute x22, waiting for transfers between devices, shift(): lax.ppermute(x, 'dap', [((c + by) % chips * cores + s, c * cores + s) for...  1130 us
    pallas_call x16, Pallas kernels, mix(): pl.pallas_call(functools.partial(mix_kernel, pieces, half, len(args)), gr...  706 us
    pallas_call x12, Pallas kernels, project(): pl.pallas_call(functools.partial(project_kernel, len(z_parts), sides), gr...  598 us
    ppermute x16, waiting for transfers between devices, swap(): return lax.ppermute(x, 'dap', [(i, i ^ 1) for i in range(group)])  136 us
  transfers between devices with their start and end apart: 40, of which 18 were waited for; matrix products, arithmetic and copies ran while one was open for 3% of the time, Pallas kernels for 39%

profile of v1, /device:TPU:112, one launch (start us, length us, event | category | flops | bytes accessed | tf_op | source)
XLA Modules:
  0.0 2703.3 jit_solution(12753506494929568544)
XLA Ops:
  10.6 48.0 %project.13 = (bf16[128,96,768]{2,1,0:T(8,128)(2,1)}, bf16[128,96,768]{2,1,0:T(8,128)(2,1)}) custom-call(bf16[96,768,128]{2,1,0:T(8,128)(2,1)} %refs_3_.11, s32[96,768]{1,0:T(8,128)} %refs_1_.3, f32[2,128]{1,0:T(2,128)} %get-tuple-element.193.refs_2_.refs_4_, bf16[512,128]{1,0:T(8,128)(2,1)} %get-tuple-element.197.refs_3_), custom_call_target="tpu_custom_call" | custom-call | flops 10000000 | bytes 56623104 | tf_op jit(solution)/shard_map/project/pallas_call | solution.py:87
  58.6 48.0 %project.12 = (bf16[128,96,768]{2,1,0:T(8,128)(2,1)}, bf16[128,96,768]{2,1,0:T(8,128)(2,1)}) custom-call(bf16[96,768,128]{2,1,0:T(8,128)(2,1)} %refs_3_.10, s32[96,768]{1,0:T(8,128)} %refs_1_.2, f32[2,128]{1,0:T(2,128)} %get-tuple-element.193.refs_2_.refs_4_, bf16[512,128]{1,0:T(8,128)(2,1)} %get-tuple-element.197.refs_3_), custom_call_target="tpu_custom_call" | custom-call | flops 10000000 | bytes 56623104 | tf_op jit(solution)/shard_map/project/pallas_call | solution.py:87
  114.6 44.4 %mix.17.refs_4_ = bf16[96,192,128]{2,1,0:T(8,128)(2,1)} custom-call(s32[3]{0:T(128)} %fusion.12.info, bf16[128,96,768]{2,1,0:T(8,128)(2,1)} %get-tuple-element.81.refs_0_, bf16[128,96,768]{2,1,0:T(8,128)(2,1)} %get-tuple-element.82.refs_1_, bf16[128,96,768]{2,1,0:T(8,128)(2,1)} %collective-permute-done.3.refs_2_, bf16[96,768,128]{2,1,0:T(8,128)(2,1)} %refs_3_.11, ...), custom_call_target="tpu_custom_call" | custom-call | flops 9000000 | bytes 56623104 | tf_op jit(solution)/shard_map/mix/pallas_call | solution.py:166
  159.0 44.2 %mix.16.refs_4_ = bf16[96,192,128]{2,1,0:T(8,128)(2,1)} custom-call(s32[3]{0:T(128)} %fusion.12.info, bf16[128,96,768]{2,1,0:T(8,128)(2,1)} %get-tuple-element.79.refs_0_, bf16[128,96,768]{2,1,0:T(8,128)(2,1)} %get-tuple-element.80.refs_1_, bf16[128,96,768]{2,1,0:T(8,128)(2,1)} %collective-permute-done.2.refs_2_, bf16[96,768,128]{2,1,0:T(8,128)(2,1)} %refs_3_.10, ...), custom_call_target="tpu_custom_call" | custom-call | flops 9000000 | bytes 56623104 | tf_op jit(solution)/shard_map/mix/pallas_call | solution.py:166
  203.2 331.6 %collective-permute-done.refs_0_.refs_3_ = bf16[96,768,128]{2,1,0:T(8,128)(2,1)} collective-permute-done((bf16[96,768,128]{2,1,0:T(8,128)(2,1)}, bf16[96,768,128]{2,1,0:T(8,128)(2,1)}, u32[]{:S(2)}, u32[]{:S(2)}) %collective-permute-start) | collective-permute-done | bytes 18874400 | tf_op jit(solution)/shard_map/ppermute | solution.py:187
  540.1 48.0 %project.15 = (bf16[128,96,768]{2,1,0:T(8,128)(2,1)}, bf16[128,96,768]{2,1,0:T(8,128)(2,1)}) custom-call(bf16[96,768,128]{2,1,0:T(8,128)(2,1)} %collective-permute-done.1.refs_0_.refs_3_, s32[96,768]{1,0:T(8,128)} %get-tuple-element.181.refs_1_, f32[2,128]{1,0:T(2,128)} %get-tuple-element.193.refs_2_.refs_4_, bf16[512,128]{1,0:T(8,128)(2,1)} %get-tuple-element.197.refs_3_), custom_call_target="tpu_custom_call" | custom-call | flops 10000000 | bytes 56623104 | tf_op jit(solution)/shard_map/project/pallas_call | solution.py:87
  590.1 47.9 %project.14 = (bf16[128,96,768]{2,1,0:T(8,128)(2,1)}, bf16[128,96,768]{2,1,0:T(8,128)(2,1)}) custom-call(bf16[96,768,128]{2,1,0:T(8,128)(2,1)} %collective-permute-done.refs_0_.refs_3_, s32[96,768]{1,0:T(8,128)} %get-tuple-element.183.refs_1_, f32[2,128]{1,0:T(2,128)} %get-tuple-element.193.refs_2_.refs_4_, bf16[512,128]{1,0:T(8,128)(2,1)} %get-tuple-element.197.refs_3_), custom_call_target="tpu_custom_call" | custom-call | flops 10000000 | bytes 56623104 | tf_op jit(solution)/shard_map/project/pallas_call | solution.py:87
  695.2 44.5 %mix.18.refs_4_ = bf16[96,192,128]{2,1,0:T(8,128)(2,1)} custom-call(s32[3]{0:T(128)} %fusion.12.info, bf16[128,96,768]{2,1,0:T(8,128)(2,1)} %get-tuple-element.86.refs_0_, bf16[128,96,768]{2,1,0:T(8,128)(2,1)} %get-tuple-element.80.refs_1_, bf16[128,96,768]{2,1,0:T(8,128)(2,1)} %collective-permute-done.2.refs_2_, ...), custom_call_target="tpu_custom_call" | custom-call | flops 9000000 | bytes 56623104 | tf_op jit(solution)/shard_map/mix/pallas_call | solution.py:166
  760.0 44.2 %mix.21.refs_4_ = bf16[96,192,128]{2,1,0:T(8,128)(2,1)} custom-call(s32[3]{0:T(128)} %fusion.15.info, bf16[128,96,768]{2,1,0:T(8,128)(2,1)} %get-tuple-element.81.refs_0_, bf16[128,96,768]{2,1,0:T(8,128)(2,1)} %get-tuple-element.92.refs_1_, bf16[128,96,768]{2,1,0:T(8,128)(2,1)} %collective-permute-done.11.refs_2_, bf16[96,768,128]{2,1,0:T(8,128)(2,1)} %refs_3_.11, ...), custom_call_target="tpu_custom_call" | custom-call | flops 9000000 | bytes 56623104 | tf_op jit(solution)/shard_map/mix/pallas_call | solution.py:166
  863.5 183.7 %collective-permute-done.10.refs_0_ = bf16[96,768,128]{2,1,0:T(8,128)(2,1)} collective-permute-done((bf16[96,768,128]{2,1,0:T(8,128)(2,1)}, bf16[96,768,128]{2,1,0:T(8,128)(2,1)}, u32[]{:S(2)}, u32[]{:S(2)}) %collective-permute-start.10) | collective-permute-done | bytes 18874400 | tf_op jit(solution)/shard_map/ppermute | solution.py:187
  1234.6 96.0 %collective-permute-done.4.refs_1_ = bf16[192,96,128]{2,1,0:T(8,128)(2,1)} collective-permute-done((bf16[192,96,128]{2,1,0:T(8,128)(2,1)}, bf16[192,96,128]{2,1,0:T(8,128)(2,1)}, u32[]{:S(2)}, u32[]{:S(2)}) %collective-permute-start.4) | collective-permute-done | bytes 4718624 | tf_op jit(solution)/shard_map/ppermute | solution.py:187
  1330.6 100.2 %collective-permute-done.7.refs_1_ = bf16[192,96,128]{2,1,0:T(8,128)(2,1)} collective-permute-done((bf16[192,96,128]{2,1,0:T(8,128)(2,1)}, bf16[192,96,128]{2,1,0:T(8,128)(2,1)}, u32[]{:S(2)}, u32[]{:S(2)}) %collective-permute-start.7) | collective-permute-done | bytes 4718624 | tf_op jit(solution)/shard_map/ppermute | solution.py:187
  1434.3 56.2 %project.18 = (bf16[128,192,384]{2,1,0:T(8,128)(2,1)}, bf16[128,192,384]{2,1,0:T(8,128)(2,1)}) custom-call(bf16[192,96,128]{2,1,0:T(8,128)(2,1)} %bitcast.129, bf16[192,96,128]{2,1,0:T(8,128)(2,1)} %collective-permute-done.4.refs_1_, bf16[192,96,128]{2,1,0:T(8,128)(2,1)} %collective-permute-done.5.refs_2_, ...), custom_call_target="tpu_custom_call" | custom-call | flops 10000000 | bytes 56623104 | tf_op jit(solution)/shard_map/project/pallas_call | solution.py:87
  1490.5 45.4 %collective-permute-done.17.refs_2_ = bf16[192,96,128]{2,1,0:T(8,128)(2,1)} collective-permute-done((bf16[192,96,128]{2,1,0:T(8,128)(2,1)}, bf16[192,96,128]{2,1,0:T(8,128)(2,1)}, u32[]{:S(2)}, u32[]{:S(2)}) %collective-permute-start.17) | collective-permute-done | bytes 4718624 | tf_op jit(solution)/shard_map/ppermute | solution.py:187
  1535.9 56.2 %project.19 = (bf16[128,192,384]{2,1,0:T(8,128)(2,1)}, bf16[128,192,384]{2,1,0:T(8,128)(2,1)}) custom-call(bf16[192,96,128]{2,1,0:T(8,128)(2,1)} %bitcast.126, bf16[192,96,128]{2,1,0:T(8,128)(2,1)} %bitcast.124, bf16[192,96,128]{2,1,0:T(8,128)(2,1)} %collective-permute-done.17.refs_2_, bf16[192,96,128]{2,1,0:T(8,128)(2,1)} %collective-permute-done.8.refs_3_, ...), custom_call_target="tpu_custom_call" | custom-call | flops 10000000 | bytes 56623104 | tf_op jit(solution)/shard_map/project/pallas_call | solution.py:87
  1706.1 44.4 %mix.24 = bf16[96,192,128]{2,1,0:T(8,128)(2,1)} custom-call(s32[3]{0:T(128)} %pad.30.info, bf16[128,192,384]{2,1,0:T(8,128)(2,1)} %get-tuple-element.121.refs_0_, bf16[128,192,384]{2,1,0:T(8,128)(2,1)} %collective-permute-done.26.refs_1_, bf16[128,192,384]{2,1,0:T(8,128)(2,1)} %get-tuple-element.120.refs_2_, ...), custom_call_target="tpu_custom_call" | custom-call | flops 9000000 | bytes 56623104 | tf_op jit(solution)/shard_map/mix/pallas_call | solution.py:166
  1838.5 89.8 %collective-permute-done.21.refs_1_ = bf16[192,96,128]{2,1,0:T(8,128)(2,1)} collective-permute-done((bf16[192,96,128]{2,1,0:T(8,128)(2,1)}, bf16[192,96,128]{2,1,0:T(8,128)(2,1)}, u32[]{:S(2)}, u32[]{:S(2)}) %collective-permute-start.21) | collective-permute-done | bytes 4718624 | tf_op jit(solution)/shard_map/ppermute | solution.py:187
  1928.3 52.6 %project.20.refs_2_ = bf16[128,192,384]{2,1,0:T(8,128)(2,1)} custom-call(bf16[192,96,128]{2,1,0:T(8,128)(2,1)} %bitcast.107.refs_0_, bf16[192,96,128]{2,1,0:T(8,128)(2,1)} %collective-permute-done.7.refs_1_, bf16[192,96,128]{2,1,0:T(8,128)(2,1)} %collective-permute-done.22.refs_2_, bf16[192,96,128]{2,1,0:T(8,128)(2,1)} %collective-permute-done.23.refs_3_, ...), custom_call_target="tpu_custom_call" | custom-call | flops 8000000 | bytes 37748736 | tf_op jit(solution)/shard_map/project/pallas_call | solution.py:87
  2086.0 100.6 %collective-permute-done.16.refs_3_ = bf16[192,96,128]{2,1,0:T(8,128)(2,1)} collective-permute-done((bf16[192,96,128]{2,1,0:T(8,128)(2,1)}, bf16[192,96,128]{2,1,0:T(8,128)(2,1)}, u32[]{:S(2)}, u32[]{:S(2)}) %collective-permute-start.16) | collective-permute-done | bytes 4718624 | tf_op jit(solution)/shard_map/ppermute | solution.py:187
  2192.1 56.2 %project.21 = (bf16[128,192,384]{2,1,0:T(8,128)(2,1)}, bf16[128,192,384]{2,1,0:T(8,128)(2,1)}) custom-call(bf16[192,96,128]{2,1,0:T(8,128)(2,1)} %bitcast.122, bf16[192,96,128]{2,1,0:T(8,128)(2,1)} %collective-permute-done.19.refs_1_, bf16[192,96,128]{2,1,0:T(8,128)(2,1)} %collective-permute-done.20.refs_2_, ...), custom_call_target="tpu_custom_call" | custom-call | flops 10000000 | bytes 56623104 | tf_op jit(solution)/shard_map/project/pallas_call | solution.py:87
  2290.1 56.2 %project.22 = (bf16[128,192,384]{2,1,0:T(8,128)(2,1)}, bf16[128,192,384]{2,1,0:T(8,128)(2,1)}) custom-call(bf16[192,96,128]{2,1,0:T(8,128)(2,1)} %bitcast.119, bf16[192,96,128]{2,1,0:T(8,128)(2,1)} %bitcast.117, bf16[192,96,128]{2,1,0:T(8,128)(2,1)} %collective-permute-done.29.refs_2_, bf16[192,96,128]{2,1,0:T(8,128)(2,1)} %collective-permute-done.15.refs_3_, ...), custom_call_target="tpu_custom_call" | custom-call | flops 10000000 | bytes 56623104 | tf_op jit(solution)/shard_map/project/pallas_call | solution.py:87
  2346.3 47.6 %collective-permute-done.31.refs_3_ = bf16[192,96,128]{2,1,0:T(8,128)(2,1)} collective-permute-done((bf16[192,96,128]{2,1,0:T(8,128)(2,1)}, bf16[192,96,128]{2,1,0:T(8,128)(2,1)}, u32[]{:S(2)}, u32[]{:S(2)}) %collective-permute-start.31) | collective-permute-done | bytes 4718624 | tf_op jit(solution)/shard_map/ppermute | solution.py:187
  2394.9 52.6 %project.23.refs_2_ = bf16[128,192,384]{2,1,0:T(8,128)(2,1)} custom-call(bf16[192,96,128]{2,1,0:T(8,128)(2,1)} %bitcast.131, bf16[192,96,128]{2,1,0:T(8,128)(2,1)} %collective-permute-done.21.refs_1_, bf16[192,96,128]{2,1,0:T(8,128)(2,1)} %collective-permute-done.30.refs_2_, bf16[192,96,128]{2,1,0:T(8,128)(2,1)} %collective-permute-done.31.refs_3_, ...), custom_call_target="tpu_custom_call" | custom-call | flops 8000000 | bytes 37748736 | tf_op jit(solution)/shard_map/project/pallas_call | solution.py:87
  2495.9 57.4 %collective-permute-done.28 = bf16[96,192,128]{2,1,0:T(8,128)(2,1)} collective-permute-done((bf16[96,192,128]{2,1,0:T(8,128)(2,1)}, bf16[96,192,128]{2,1,0:T(8,128)(2,1)}, u32[]{:S(2)}, u32[]{:S(2)}) %collective-permute-start.28) | collective-permute-done | bytes 4718624 | tf_op jit(solution)/shard_map/ppermute | solution.py:187
  (140 shorter events, 893.0 us)
Async XLA Ops:
  7.2 196.0 %all-gather.3.cloned.1.call-start = ((), (), s32[]{:S(2)}) async-start(), calls=%async_computation | async-start | bytes 2654208 | tf_op jit(solution)/shard_map/all_gather | solution.py:225
  107.1 427.7 %collective-permute-start = (bf16[96,768,128]{2,1,0:T(8,128)(2,1)}, bf16[96,768,128]{2,1,0:T(8,128)(2,1)}, u32[]{:S(2)}, u32[]{:S(2)}) collective-permute-start(bf16[96,768,128]{2,1,0:T(8,128)(2,1)} %refs_3_.10), channel_id=1, source_target_pairs={{2,0},{3,1},{4,2},{5,3},{6,4},{7,5},{0,6},{1,7},{10,8},{11,9},{12,... | collective-permute-start | bytes 56623112 | tf_op jit(solution)/shard_map/ppermute | solution.py:187
  110.9 427.3 %collective-permute-start.1 = (bf16[96,768,128]{2,1,0:T(8,128)(2,1)}, bf16[96,768,128]{2,1,0:T(8,128)(2,1)}, u32[]{:S(2)}, u32[]{:S(2)}) collective-permute-start(bf16[96,768,128]{2,1,0:T(8,128)(2,1)} %refs_3_.11), channel_id=1, source_target_pairs={{6,0},{7,1},{0,2},{1,3},{2,4},{3,5},{4,6},{5,7},{14,8},{15,9},{8,1... | collective-permute-start | bytes 56623112 | tf_op jit(solution)/shard_map/ppermute | solution.py:187
  588.2 171.9 %collective-permute-start.11 = (bf16[128,96,768]{2,1,0:T(8,128)(2,1)}, bf16[128,96,768]{2,1,0:T(8,128)(2,1)}, u32[]{:S(2)}, u32[]{:S(2)}) collective-permute-start(bf16[128,96,768]{2,1,0:T(8,128)(2,1)} %get-tuple-element.92.refs_1_), channel_id=1, source_target_pairs={{0,1},{1,0},{2,3},{3,2},{4,5},{5,4},{6,7},{7,6},{8,9},{9,8},{10,11... | collective-permute-start | bytes 56623112 | tf_op jit(solution)/shard_map/ppermute | solution.py:190
  638.0 173.8 %collective-permute-start.6 = (bf16[128,96,768]{2,1,0:T(8,128)(2,1)}, bf16[128,96,768]{2,1,0:T(8,128)(2,1)}, u32[]{:S(2)}, u32[]{:S(2)}) collective-permute-start(bf16[128,96,768]{2,1,0:T(8,128)(2,1)} %get-tuple-element.87.refs_1_), channel_id=1, source_target_pairs={{0,1},{1,0},{2,3},{3,2},{4,5},{5,4},{6,7},{7,6},{8,9},{9,8},{10,11... | collective-permute-start | bytes 56623112 | tf_op jit(solution)/shard_map/ppermute | solution.py:190
  638.5 408.7 %collective-permute-start.10 = (bf16[96,768,128]{2,1,0:T(8,128)(2,1)}, bf16[96,768,128]{2,1,0:T(8,128)(2,1)}, u32[]{:S(2)}, u32[]{:S(2)}) collective-permute-start(bf16[96,768,128]{2,1,0:T(8,128)(2,1)} %collective-permute-done.1.refs_0_.refs_3_), channel_id=1, source_target_pairs={{6,0},{7,1},{0,2},{1,3},{2,4},{3,5},{4,6},{5,7},{14,8},{15,9},{8,1... | collective-permute-start | bytes 56623112 | tf_op jit(solution)/shard_map/ppermute | solution.py:187
  638.5 408.7 %collective-permute-start.9 = (bf16[96,768,128]{2,1,0:T(8,128)(2,1)}, bf16[96,768,128]{2,1,0:T(8,128)(2,1)}, u32[]{:S(2)}, u32[]{:S(2)}) collective-permute-start(bf16[96,768,128]{2,1,0:T(8,128)(2,1)} %collective-permute-done.refs_0_.refs_3_), channel_id=1, source_target_pairs={{2,0},{3,1},{4,2},{5,3},{6,4},{7,5},{0,6},{1,7},{10,8},{11,9},{12,... | collective-permute-start | bytes 56623112 | tf_op jit(solution)/shard_map/ppermute | solution.py:187
  1124.0 110.6 %collective-permute-start.5 = (bf16[192,96,128]{2,1,0:T(8,128)(2,1)}, bf16[192,96,128]{2,1,0:T(8,128)(2,1)}, u32[]{:S(2)}, u32[]{:S(2)}) collective-permute-start(bf16[192,96,128]{2,1,0:T(8,128)(2,1)} %bitcast.123), channel_id=1, source_target_pairs={{2,0},{3,1},{4,2},{5,3},{6,4},{7,5},{0,6},{1,7},{10,8},{11,9},{12,... | collective-permute-start | bytes 14155784 | tf_op jit(solution)/shard_map/ppermute | solution.py:187
  1127.0 203.6 %collective-permute-start.4 = (bf16[192,96,128]{2,1,0:T(8,128)(2,1)}, bf16[192,96,128]{2,1,0:T(8,128)(2,1)}, u32[]{:S(2)}, u32[]{:S(2)}) collective-permute-start(bf16[192,96,128]{2,1,0:T(8,128)(2,1)} %bitcast.125), channel_id=1, source_target_pairs={{2,0},{3,1},{4,2},{5,3},{6,4},{7,5},{0,6},{1,7},{10,8},{11,9},{12,... | collective-permute-start | bytes 14155784 | tf_op jit(solution)/shard_map/ppermute | solution.py:187
  1127.0 303.8 %collective-permute-start.7 = (bf16[192,96,128]{2,1,0:T(8,128)(2,1)}, bf16[192,96,128]{2,1,0:T(8,128)(2,1)}, u32[]{:S(2)}, u32[]{:S(2)}) collective-permute-start(bf16[192,96,128]{2,1,0:T(8,128)(2,1)} %bitcast.127), channel_id=1, source_target_pairs={{2,0},{3,1},{4,2},{5,3},{6,4},{7,5},{0,6},{1,7},{10,8},{11,9},{12,... | collective-permute-start | bytes 14155784 | tf_op jit(solution)/shard_map/ppermute | solution.py:187
  1127.0 303.7 %collective-permute-start.8 = (bf16[192,96,128]{2,1,0:T(8,128)(2,1)}, bf16[192,96,128]{2,1,0:T(8,128)(2,1)}, u32[]{:S(2)}, u32[]{:S(2)}) collective-permute-start(bf16[192,96,128]{2,1,0:T(8,128)(2,1)} %bitcast.128), channel_id=1, source_target_pairs={{6,0},{7,1},{0,2},{1,3},{2,4},{3,5},{4,6},{5,7},{14,8},{15,9},{8,1... | collective-permute-start | bytes 14155784 | tf_op jit(solution)/shard_map/ppermute | solution.py:187
  1180.6 250.1 %collective-permute-start.13 = (bf16[192,96,128]{2,1,0:T(8,128)(2,1)}, bf16[192,96,128]{2,1,0:T(8,128)(2,1)}, u32[]{:S(2)}, u32[]{:S(2)}) collective-permute-start(bf16[192,96,128]{2,1,0:T(8,128)(2,1)} %bitcast.107.refs_0_), channel_id=1, source_target_pairs={{6,0},{7,1},{0,2},{1,3},{2,4},{3,5},{4,6},{5,7},{14,8},{15,9},{8,1... | collective-permute-start | bytes 14155784 | tf_op jit(solution)/shard_map/ppermute | solution.py:187
  1593.2 335.1 %collective-permute-start.22 = (bf16[192,96,128]{2,1,0:T(8,128)(2,1)}, bf16[192,96,128]{2,1,0:T(8,128)(2,1)}, u32[]{:S(2)}, u32[]{:S(2)}) collective-permute-start(bf16[192,96,128]{2,1,0:T(8,128)(2,1)} %collective-permute-done.4.refs_1_), channel_id=1, source_target_pairs={{2,0},{3,1},{4,2},{5,3},{6,4},{7,5},{0,6},{1,7},{10,8},{11,9},{12,... | collective-permute-start | bytes 14155784 | tf_op jit(solution)/shard_map/ppermute | solution.py:187
  1620.7 217.8 %collective-permute-start.19 = (bf16[192,96,128]{2,1,0:T(8,128)(2,1)}, bf16[192,96,128]{2,1,0:T(8,128)(2,1)}, u32[]{:S(2)}, u32[]{:S(2)}) collective-permute-start(bf16[192,96,128]{2,1,0:T(8,128)(2,1)} %bitcast.118), channel_id=1, source_target_pairs={{6,0},{7,1},{0,2},{1,3},{2,4},{3,5},{4,6},{5,7},{14,8},{15,9},{8,1... | collective-permute-start | bytes 14155784 | tf_op jit(solution)/shard_map/ppermute | solution.py:187
  1647.7 190.8 %collective-permute-start.20 = (bf16[192,96,128]{2,1,0:T(8,128)(2,1)}, bf16[192,96,128]{2,1,0:T(8,128)(2,1)}, u32[]{:S(2)}, u32[]{:S(2)}) collective-permute-start(bf16[192,96,128]{2,1,0:T(8,128)(2,1)} %bitcast.116), channel_id=1, source_target_pairs={{6,0},{7,1},{0,2},{1,3},{2,4},{3,5},{4,6},{5,7},{14,8},{15,9},{8,1... | collective-permute-start | bytes 14155784 | tf_op jit(solution)/shard_map/ppermute | solution.py:187
  1674.6 253.6 %collective-permute-start.21 = (bf16[192,96,128]{2,1,0:T(8,128)(2,1)}, bf16[192,96,128]{2,1,0:T(8,128)(2,1)}, u32[]{:S(2)}, u32[]{:S(2)}) collective-permute-start(bf16[192,96,128]{2,1,0:T(8,128)(2,1)} %bitcast.120), channel_id=1, source_target_pairs={{6,0},{7,1},{0,2},{1,3},{2,4},{3,5},{4,6},{5,7},{14,8},{15,9},{8,1... | collective-permute-start | bytes 14155784 | tf_op jit(solution)/shard_map/ppermute | solution.py:187
  1701.6 226.6 %collective-permute-start.23 = (bf16[192,96,128]{2,1,0:T(8,128)(2,1)}, bf16[192,96,128]{2,1,0:T(8,128)(2,1)}, u32[]{:S(2)}, u32[]{:S(2)}) collective-permute-start(bf16[192,96,128]{2,1,0:T(8,128)(2,1)} %collective-permute-done.5.refs_2_), channel_id=1, source_target_pairs={{2,0},{3,1},{4,2},{5,3},{6,4},{7,5},{0,6},{1,7},{10,8},{11,9},{12,... | collective-permute-start | bytes 14155784 | tf_op jit(solution)/shard_map/ppermute | solution.py:187
  1981.5 205.0 %collective-permute-start.16 = (bf16[192,96,128]{2,1,0:T(8,128)(2,1)}, bf16[192,96,128]{2,1,0:T(8,128)(2,1)}, u32[]{:S(2)}, u32[]{:S(2)}) collective-permute-start(bf16[192,96,128]{2,1,0:T(8,128)(2,1)} %bitcast.130), channel_id=1, source_target_pairs={{2,0},{3,1},{4,2},{5,3},{6,4},{7,5},{0,6},{1,7},{10,8},{11,9},{12,... | collective-permute-start | bytes 14155784 | tf_op jit(solution)/shard_map/ppermute | solution.py:187
  2188.3 158.0 %collective-permute-start.30 = (bf16[192,96,128]{2,1,0:T(8,128)(2,1)}, bf16[192,96,128]{2,1,0:T(8,128)(2,1)}, u32[]{:S(2)}, u32[]{:S(2)}) collective-permute-start(bf16[192,96,128]{2,1,0:T(8,128)(2,1)} %collective-permute-done.19.refs_1_), channel_id=1, source_target_pairs={{6,0},{7,1},{0,2},{1,3},{2,4},{3,5},{4,6},{5,7},{14,8},{15,9},{8,1... | collective-permute-start | bytes 14155784 | tf_op jit(solution)/shard_map/ppermute | solution.py:187
  2188.6 205.3 %collective-permute-start.31 = (bf16[192,96,128]{2,1,0:T(8,128)(2,1)}, bf16[192,96,128]{2,1,0:T(8,128)(2,1)}, u32[]{:S(2)}, u32[]{:S(2)}) collective-permute-start(bf16[192,96,128]{2,1,0:T(8,128)(2,1)} %collective-permute-done.20.refs_2_), channel_id=1, source_target_pairs={{6,0},{7,1},{0,2},{1,3},{2,4},{3,5},{4,6},{5,7},{14,8},{15,9},{8,1... | collective-permute-start | bytes 14155784 | tf_op jit(solution)/shard_map/ppermute | solution.py:187
  2394.4 164.2 %collective-permute-start.32 = (bf16[128,192,384]{2,1,0:T(8,128)(2,1)}, bf16[128,192,384]{2,1,0:T(8,128)(2,1)}, u32[]{:S(2)}, u32[]{:S(2)}) collective-permute-start(bf16[128,192,384]{2,1,0:T(8,128)(2,1)} %get-tuple-element.145.refs_0_), channel_id=1, source_target_pairs={{0,1},{1,0},{2,3},{3,2},{4,5},{5,4},{6,7},{7,6},{8,9},{9,8},{10,11... | collective-permute-start | bytes 56623112 | tf_op jit(solution)/shard_map/ppermute | solution.py:190
  2394.4 208.4 %collective-permute-start.34 = (bf16[128,192,384]{2,1,0:T(8,128)(2,1)}, bf16[128,192,384]{2,1,0:T(8,128)(2,1)}, u32[]{:S(2)}, u32[]{:S(2)}) collective-permute-start(bf16[128,192,384]{2,1,0:T(8,128)(2,1)} %get-tuple-element.151.refs_2_), channel_id=1, source_target_pairs={{0,1},{1,0},{2,3},{3,2},{4,5},{5,4},{6,7},{7,6},{8,9},{9,8},{10,11... | collective-permute-start | bytes 56623112 | tf_op jit(solution)/shard_map/ppermute | solution.py:190
  2447.5 199.4 %collective-permute-start.33 = (bf16[128,192,384]{2,1,0:T(8,128)(2,1)}, bf16[128,192,384]{2,1,0:T(8,128)(2,1)}, u32[]{:S(2)}, u32[]{:S(2)}) collective-permute-start(bf16[128,192,384]{2,1,0:T(8,128)(2,1)} %project.23.refs_2_), channel_id=1, source_target_pairs={{0,1},{1,0},{2,3},{3,2},{4,5},{5,4},{6,7},{7,6},{8,9},{9,8},{10,11... | collective-permute-start | bytes 56623112 | tf_op jit(solution)/shard_map/ppermute | solution.py:190
  2493.2 197.7 %collective-permute-start.37 = (bf16[96,192,128]{2,1,0:T(8,128)(2,1)}, bf16[96,192,128]{2,1,0:T(8,128)(2,1)}, u32[]{:S(2)}, u32[]{:S(2)}) collective-permute-start(bf16[96,192,128]{2,1,0:T(8,128)(2,1)} %mix.28), channel_id=1, source_target_pairs={{2,0},{3,1},{4,2},{5,3},{6,4},{7,5},{0,6},{1,7},{10,8},{11,9},{12,... | collective-permute-start | bytes 14155784 | tf_op jit(solution)/shard_map/ppermute | solution.py:187
  (22 other events, 1732.3 us)
Sparse Core Ops, SparseCore 0:
  111.1 32.1 all-gather.2
  144.8 29.7 all-gather.4

commit v2 on v1

--- a/solution.py
+++ b/solution.py
@@ -147,7 +147,7 @@
     hidden, _, depth = a_parts[0].shape
     half = b_parts[0].shape[1] // (1 if pieces == 1 else 2)
     cols, width = 2 * half, z.shape[2]
-    chunk = 8
+    chunk = 16
     pick = (lambda c, s: (c, 0, 0)) if pieces == 1 else (lambda c, s: (c, s[2], 0))
     zero = jnp.zeros((), jnp.int32)
     info = jnp.stack([col_block, zero if dest is None else dest, core]).astype(jnp.int32)
@@ -210,30 +210,25 @@
         def at(n, ahead):
             return (chip + turns[n] * ahead) % chips
 
-        def mask_rows(n, ahead):
-            return lax.dynamic_slice_in_dim(whole_mask[n], (at(n, ahead) * cores + core) * rows, rows, 0)
-
         def mask_cols(n, ahead):
-            strip = lax.dynamic_slice_in_dim(mask_t[n], at(n, ahead) * cols, cols, 0)
-            return [lax.dynamic_slice_in_dim(strip, (at(n, r) * cores + core) * rows, rows, 1) for r in range(chips)]
+            return [lax.dynamic_slice_in_dim(masks[n][r], at(n, ahead) * cols, cols, 1).T for r in range(chips)]
 
         turned = lambda x: jnp.swapaxes(x, 0, 1)
         tie = lax.optimization_barrier
 
         par, fin = weights(0)
         z1 = [shift(z0[n], turns[n]) for n in crops]
-        whole_mask = [lax.all_gather(m, "dap", axis=0, tiled=True) for m in mask]
+        masks = [[mask[n]] + [shift(mask[n], turns[n] * r) for r in (1, 2, -1)] for n in crops]
         ab0 = [project([z0[n]], [mask[n]], *par, 2) for n in crops]
         b0s = [swap(ab0[n][1]) for n in crops]
         x00 = [mix([ab0[n][0]], [ab0[n][1], b0s[n]], z0[n], at(n, 0), core, *fin) for n in crops]
-        z1, x00, whole_mask = tie((z1, x00, whole_mask))
+        z1, x00, masks = tie((z1, x00, masks))
         z2 = [shift(z1[n], turns[n]) for n in crops]
-        ab1 = [project([z1[n]], [mask_rows(n, 1)], *par, 2) for n in crops]
+        ab1 = [project([z1[n]], [masks[n][1]], *par, 2) for n in crops]
         b1s = [swap(ab1[n][1]) for n in crops]
         x10 = [mix([ab1[n][0]], [ab0[n][1], b0s[n]], z1[n], at(n, 0), core, *fin) for n in crops]
         x01 = [mix([ab0[n][0]], [ab1[n][1], b1s[n]], z0[n], at(n, 1), core, *fin) for n in crops]
         t00, t10, t01 = [[turned(x[n]) for n in crops] for x in (x00, x10, x01)]
-        mask_t = [m.T for m in whole_mask]
 
         first, second = crops
         l1 = [shift(x[first], turns[first]) for x in (t00, t10, t01)]
@@ -241,7 +236,7 @@
         z2, t00, t10, t01 = tie((z2, t00, t10, t01))
         b2, b2s, x02, t02 = [None] * 2, [None] * 2, [None] * 2, [None] * 2
         for n in crops:
-            b2[n], = project([z2[n]], [mask_rows(n, 2)], *par, 1)
+            b2[n], = project([z2[n]], [masks[n][2]], *par, 1)
             b2s[n] = swap(b2[n])
         x02[first] = mix([ab0[first][0]], [b2[first], b2s[first]], z0[first], at(first, 2), core, *fin)
         t02[first], b2[second] = tie((turned(x02[first]), b2[second]))
@@ -265,8 +260,7 @@
             (own, other), (own_b, other_b) = one, two
             return mix([own[0], other[0]], [own_b[-1], other_b[-1]], x, zero, core, *fin, **where)
 
-        l1, r1, own = tie((l1, r1, (t00[second], t10[second], t01[second], t02[second])))
-        t00[second], t10[second], t01[second], t02[second] = own
+        l1[:2], r1, x02[second] = tie((l1[:2], r1, x02[second]))
         r2 = shift(r1[1], -turns[first])
         l2 = [shift(x, turns[first]) for x in l1[:2]]
         m1 = [shift(x[second], turns[second]) for x in (t00, t10, t01)]
@@ -282,9 +276,10 @@
         out, y10 = tie((x00[n], y10))
         out = turn_block(c0, c0, out, whole=cols * chips, dest=at(n, 0))
         out = turn_block(c0, c1, x01[n], whole=out, dest=at(n, 1))
-        m1, col2, out = tie((m1, col2, out))
+        col2, out = tie((col2, out))
+        c2 = both(column(n, 2, col2))
+        m1, out = tie((m1, out))
         m2 = [shift(x, turns[second]) for x in m1[:2]]
-        c2 = both(column(n, 2, col2))
         out = turn_block(c0, c2, x02[n], whole=out, dest=at(n, 2))
         s1, out, m1 = tie((s1, out, m1))
         s2 = shift(s1[1], -turns[second])

time: 2710 us -> 2790 us (1.030)
  waiting for transfers between devices: 1270 us -> 1420 us
  Pallas kernels: 1300 us -> 1240 us
    ppermute x22 -> x28, waiting for transfers between devices: 1130 us -> 1360 us  [shift(): lax.ppermute(x, 'dap', [((c + by) % chips * cores + s, c * cores + s) for...]
    ppermute x16, waiting for transfers between devices: 136 us -> 55.6 us  [swap(): return lax.ppermute(x, 'dap', [(i, i ^ 1) for i in range(group)])]
    pallas_call x16, Pallas kernels: 706 us -> 640 us  [mix(): pl.pallas_call(functools.partial(mix_kernel, pieces, half, len(args)), gr...]
  transfers between devices with their start and end apart: 40 -> 44, of which waited for: 18 -> 20; matrix products, arithmetic and copies ran while one was open for 3% -> 3% of each run, Pallas kernels for 39% -> 36%
where the time goes in v2:
time: 2790 us; the launch traced here: 2780 us
  waiting for transfers between devices  1420 us (51%)
  Pallas kernels  1240 us (44%)
  local copies, waits for them, and re-layouts  85.5 us (3%)
  starting transfers between devices  31.7 us (1%)
    ppermute x28, waiting for transfers between devices, shift(): lax.ppermute(x, 'dap', [((c + by) % chips * cores + s, c * cores + s) for...  1360 us
    pallas_call x16, Pallas kernels, mix(): pl.pallas_call(functools.partial(mix_kernel, pieces, half, len(args)), gr...  640 us
    pallas_call x12, Pallas kernels, project(): pl.pallas_call(functools.partial(project_kernel, len(z_parts), sides), gr...  598 us
  transfers between devices with their start and end apart: 44, of which 20 were waited for; matrix products, arithmetic and copies ran while one was open for 3% of the time, Pallas kernels for 36%

profile of v2, /device:TPU:112, one launch (start us, length us, event | category | flops | bytes accessed | tf_op | source)
XLA Modules:
  0.0 2784.5 jit_solution(9349918474494435345)
XLA Ops:
  4.0 48.0 %project.13 = (bf16[128,96,768]{2,1,0:T(8,128)(2,1)}, bf16[128,96,768]{2,1,0:T(8,128)(2,1)}) custom-call(bf16[96,768,128]{2,1,0:T(8,128)(2,1)} %refs_3_.11, s32[96,768]{1,0:T(8,128)} %refs_1_.3, f32[2,128]{1,0:T(2,128)} %get-tuple-element.195.refs_2_.refs_4_, bf16[512,128]{1,0:T(8,128)(2,1)} %get-tuple-element.199.refs_3_), custom_call_target="tpu_custom_call" | custom-call | flops 10000000 | bytes 56623104 | tf_op jit(solution)/shard_map/project/pallas_call | solution.py:87
  52.0 48.0 %project.12 = (bf16[128,96,768]{2,1,0:T(8,128)(2,1)}, bf16[128,96,768]{2,1,0:T(8,128)(2,1)}) custom-call(bf16[96,768,128]{2,1,0:T(8,128)(2,1)} %refs_3_.10, s32[96,768]{1,0:T(8,128)} %refs_1_.2, f32[2,128]{1,0:T(2,128)} %get-tuple-element.195.refs_2_.refs_4_, bf16[512,128]{1,0:T(8,128)(2,1)} %get-tuple-element.199.refs_3_), custom_call_target="tpu_custom_call" | custom-call | flops 10000000 | bytes 56623104 | tf_op jit(solution)/shard_map/project/pallas_call | solution.py:87
  107.8 409.8 %collective-permute-done.4 = s32[96,768]{0,1:T(8,128)S(1)} collective-permute-done((s32[96,768]{0,1:T(8,128)S(1)}, s32[96,768]{0,1:T(8,128)S(1)}, u32[]{:S(2)}, u32[]{:S(2)}) %collective-permute-start.4) | collective-permute-done | bytes 294944 | tf_op jit(solution)/shard_map/ppermute | solution.py:187
  627.2 48.0 %project.15 = (bf16[128,96,768]{2,1,0:T(8,128)(2,1)}, bf16[128,96,768]{2,1,0:T(8,128)(2,1)}) custom-call(bf16[96,768,128]{2,1,0:T(8,128)(2,1)} %collective-permute-done.1.refs_0_.refs_3_, s32[96,768]{1,0:T(8,128)} %copy.26.refs_1_, f32[2,128]{1,0:T(2,128)} %get-tuple-element.195.refs_2_.refs_4_, bf16[512,128]{1,0:T(8,128)(2,1)} %get-tuple-element.199.refs_3_), custom_call_target="tpu_custom_call" | custom-call | flops 10000000 | bytes 56623104 | tf_op jit(solution)/shard_map/project/pallas_call | solution.py:87
  676.1 47.9 %project.14 = (bf16[128,96,768]{2,1,0:T(8,128)(2,1)}, bf16[128,96,768]{2,1,0:T(8,128)(2,1)}) custom-call(bf16[96,768,128]{2,1,0:T(8,128)(2,1)} %collective-permute-done.refs_0_.refs_3_, s32[96,768]{1,0:T(8,128)} %copy.24.refs_1_, f32[2,128]{1,0:T(2,128)} %get-tuple-element.195.refs_2_.refs_4_, bf16[512,128]{1,0:T(8,128)(2,1)} %get-tuple-element.199.refs_3_), custom_call_target="tpu_custom_call" | custom-call | flops 10000000 | bytes 56623104 | tf_op jit(solution)/shard_map/project/pallas_call | solution.py:87
  728.6 40.4 %mix.19.refs_4_ = bf16[96,192,128]{2,1,0:T(8,128)(2,1)} custom-call(s32[3]{0:T(128)} %fusion.12.info, bf16[128,96,768]{2,1,0:T(8,128)(2,1)} %get-tuple-element.93.refs_0_, bf16[128,96,768]{2,1,0:T(8,128)(2,1)} %get-tuple-element.85.refs_1_, bf16[128,96,768]{2,1,0:T(8,128)(2,1)} %collective-permute-done.3.refs_2_, ...), custom_call_target="tpu_custom_call" | custom-call | flops 9000000 | bytes 56623104 | tf_op jit(solution)/shard_map/mix/pallas_call | solution.py:166
  933.0 199.1 %collective-permute-done.10.refs_0_ = bf16[96,768,128]{2,1,0:T(8,128)(2,1)} collective-permute-done((bf16[96,768,128]{2,1,0:T(8,128)(2,1)}, bf16[96,768,128]{2,1,0:T(8,128)(2,1)}, u32[]{:S(2)}, u32[]{:S(2)}) %collective-permute-start.10) | collective-permute-done | bytes 18874400 | tf_op jit(solution)/shard_map/ppermute | solution.py:187
  1214.8 40.3 %mix.22.refs_4_ = bf16[96,192,128]{2,1,0:T(8,128)(2,1)} custom-call(s32[3]{0:T(128)} %fusion.16.info, bf16[128,96,768]{2,1,0:T(8,128)(2,1)} %get-tuple-element.82.refs_0_, bf16[128,96,768]{2,1,0:T(8,128)(2,1)} %project.16.refs_1_, bf16[128,96,768]{2,1,0:T(8,128)(2,1)} %collective-permute-done.15.refs_2_, bf16[96,768,128]{2,1,0:T(8,128)(2,1)} %refs_3_.10, ...), custom_call_target="tpu_custom_call" | custom-call | flops 9000000 | bytes 56623104 | tf_op jit(solution)/shard_map/mix/pallas_call | solution.py:166
  1317.2 100.2 %collective-permute-done.18.refs_1_ = bf16[192,96,128]{2,1,0:T(8,128)(2,1)} collective-permute-done((bf16[192,96,128]{2,1,0:T(8,128)(2,1)}, bf16[192,96,128]{2,1,0:T(8,128)(2,1)}, u32[]{:S(2)}, u32[]{:S(2)}) %collective-permute-start.18) | collective-permute-done | bytes 4718624 | tf_op jit(solution)/shard_map/ppermute | solution.py:187
  1422.7 56.2 %project.18 = (bf16[128,192,384]{2,1,0:T(8,128)(2,1)}, bf16[128,192,384]{2,1,0:T(8,128)(2,1)}) custom-call(bf16[192,96,128]{2,1,0:T(8,128)(2,1)} %bitcast.124, bf16[192,96,128]{2,1,0:T(8,128)(2,1)} %collective-permute-done.18.refs_1_, bf16[192,96,128]{2,1,0:T(8,128)(2,1)} %collective-permute-done.19.refs_2_, ...), custom_call_target="tpu_custom_call" | custom-call | flops 10000000 | bytes 56623104 | tf_op jit(solution)/shard_map/project/pallas_call | solution.py:87
  1478.9 44.6 %collective-permute-done.22.refs_2_ = bf16[192,96,128]{2,1,0:T(8,128)(2,1)} collective-permute-done((bf16[192,96,128]{2,1,0:T(8,128)(2,1)}, bf16[192,96,128]{2,1,0:T(8,128)(2,1)}, u32[]{:S(2)}, u32[]{:S(2)}) %collective-permute-start.22) | collective-permute-done | bytes 4718624 | tf_op jit(solution)/shard_map/ppermute | solution.py:187
  1523.5 56.3 %project.19 = (bf16[128,192,384]{2,1,0:T(8,128)(2,1)}, bf16[128,192,384]{2,1,0:T(8,128)(2,1)}) custom-call(bf16[192,96,128]{2,1,0:T(8,128)(2,1)} %bitcast.129, bf16[192,96,128]{2,1,0:T(8,128)(2,1)} %bitcast.127, bf16[192,96,128]{2,1,0:T(8,128)(2,1)} %collective-permute-done.22.refs_2_, bf16[192,96,128]{2,1,0:T(8,128)(2,1)} %collective-permute-done.20.refs_3_, ...), custom_call_target="tpu_custom_call" | custom-call | flops 10000000 | bytes 56623104 | tf_op jit(solution)/shard_map/project/pallas_call | solution.py:87
  1787.0 100.2 %collective-permute-done.26.refs_3_ = bf16[192,96,128]{2,1,0:T(8,128)(2,1)} collective-permute-done((bf16[192,96,128]{2,1,0:T(8,128)(2,1)}, bf16[192,96,128]{2,1,0:T(8,128)(2,1)}, u32[]{:S(2)}, u32[]{:S(2)}) %collective-permute-start.26) | collective-permute-done | bytes 4718624 | tf_op jit(solution)/shard_map/ppermute | solution.py:187
  1887.2 52.6 %project.20.refs_2_ = bf16[128,192,384]{2,1,0:T(8,128)(2,1)} custom-call(bf16[192,96,128]{2,1,0:T(8,128)(2,1)} %bitcast.107.refs_0_, bf16[192,96,128]{2,1,0:T(8,128)(2,1)} %collective-permute-done.24.refs_1_, bf16[192,96,128]{2,1,0:T(8,128)(2,1)} %collective-permute-done.25.refs_2_, bf16[192,96,128]{2,1,0:T(8,128)(2,1)} %collective-permute-done.26.refs_3_, ...), custom_call_target="tpu_custom_call" | custom-call | flops 8000000 | bytes 37748736 | tf_op jit(solution)/shard_map/project/pallas_call | solution.py:87
  1950.8 95.3 %collective-permute-done.31.refs_1_ = bf16[192,96,128]{2,1,0:T(8,128)(2,1)} collective-permute-done((bf16[192,96,128]{2,1,0:T(8,128)(2,1)}, bf16[192,96,128]{2,1,0:T(8,128)(2,1)}, u32[]{:S(2)}, u32[]{:S(2)}) %collective-permute-start.31) | collective-permute-done | bytes 4718624 | tf_op jit(solution)/shard_map/ppermute | solution.py:187
  2047.0 100.2 %collective-permute-done.32.refs_2_ = bf16[192,96,128]{2,1,0:T(8,128)(2,1)} collective-permute-done((bf16[192,96,128]{2,1,0:T(8,128)(2,1)}, bf16[192,96,128]{2,1,0:T(8,128)(2,1)}, u32[]{:S(2)}, u32[]{:S(2)}) %collective-permute-start.32) | collective-permute-done | bytes 4718624 | tf_op jit(solution)/shard_map/ppermute | solution.py:187
  2147.2 100.6 %collective-permute-done.33.refs_1_ = bf16[192,96,128]{2,1,0:T(8,128)(2,1)} collective-permute-done((bf16[192,96,128]{2,1,0:T(8,128)(2,1)}, bf16[192,96,128]{2,1,0:T(8,128)(2,1)}, u32[]{:S(2)}, u32[]{:S(2)}) %collective-permute-start.33) | collective-permute-done | bytes 4718624 | tf_op jit(solution)/shard_map/ppermute | solution.py:187
  2293.9 56.2 %project.21 = (bf16[128,192,384]{2,1,0:T(8,128)(2,1)}, bf16[128,192,384]{2,1,0:T(8,128)(2,1)}) custom-call(bf16[192,96,128]{2,1,0:T(8,128)(2,1)} %bitcast.122, bf16[192,96,128]{2,1,0:T(8,128)(2,1)} %collective-permute-done.31.refs_1_, bf16[192,96,128]{2,1,0:T(8,128)(2,1)} %collective-permute-done.32.refs_2_, ...), custom_call_target="tpu_custom_call" | custom-call | flops 10000000 | bytes 56623104 | tf_op jit(solution)/shard_map/project/pallas_call | solution.py:87
  2350.1 41.2 %collective-permute-done.35.refs_2_ = bf16[192,96,128]{2,1,0:T(8,128)(2,1)} collective-permute-done((bf16[192,96,128]{2,1,0:T(8,128)(2,1)}, bf16[192,96,128]{2,1,0:T(8,128)(2,1)}, u32[]{:S(2)}, u32[]{:S(2)}) %collective-permute-start.35) | collective-permute-done | bytes 4718624 | tf_op jit(solution)/shard_map/ppermute | solution.py:187
  2391.4 56.3 %project.22 = (bf16[128,192,384]{2,1,0:T(8,128)(2,1)}, bf16[128,192,384]{2,1,0:T(8,128)(2,1)}) custom-call(bf16[192,96,128]{2,1,0:T(8,128)(2,1)} %bitcast.119, bf16[192,96,128]{2,1,0:T(8,128)(2,1)} %bitcast.117, bf16[192,96,128]{2,1,0:T(8,128)(2,1)} %collective-permute-done.35.refs_2_, bf16[192,96,128]{2,1,0:T(8,128)(2,1)} %collective-permute-done.14.refs_3_, ...), custom_call_target="tpu_custom_call" | custom-call | flops 10000000 | bytes 56623104 | tf_op jit(solution)/shard_map/project/pallas_call | solution.py:87
  2447.6 46.2 %collective-permute-done.37.refs_3_ = bf16[192,96,128]{2,1,0:T(8,128)(2,1)} collective-permute-done((bf16[192,96,128]{2,1,0:T(8,128)(2,1)}, bf16[192,96,128]{2,1,0:T(8,128)(2,1)}, u32[]{:S(2)}, u32[]{:S(2)}) %collective-permute-start.37) | collective-permute-done | bytes 4718624 | tf_op jit(solution)/shard_map/ppermute | solution.py:187
  2494.8 52.9 %project.23.refs_2_ = bf16[128,192,384]{2,1,0:T(8,128)(2,1)} custom-call(bf16[192,96,128]{2,1,0:T(8,128)(2,1)} %bitcast.106.refs_0_, bf16[192,96,128]{2,1,0:T(8,128)(2,1)} %collective-permute-done.33.refs_1_, bf16[192,96,128]{2,1,0:T(8,128)(2,1)} %collective-permute-done.36.refs_2_, bf16[192,96,128]{2,1,0:T(8,128)(2,1)} %collective-permute-done.37.refs_3_, ...), custom_call_target="tpu_custom_call" | custom-call | flops 8000000 | bytes 37748736 | tf_op jit(solution)/shard_map/project/pallas_call | solution.py:87
  2592.2 61.2 %collective-permute-done.34 = bf16[96,192,128]{2,1,0:T(8,128)(2,1)} collective-permute-done((bf16[96,192,128]{2,1,0:T(8,128)(2,1)}, bf16[96,192,128]{2,1,0:T(8,128)(2,1)}, u32[]{:S(2)}, u32[]{:S(2)}) %collective-permute-start.34) | collective-permute-done | bytes 4718624 | tf_op jit(solution)/shard_map/ppermute | solution.py:187
  2698.8 40.2 %mix.30.refs_9_ = bf16[96,768,128]{2,1,0:T(8,128)(2,1)} custom-call(s32[3]{0:T(128)} %fusion.11.info, bf16[128,192,384]{2,1,0:T(8,128)(2,1)} %get-tuple-element.150.refs_0_, bf16[128,192,384]{2,1,0:T(8,128)(2,1)} %collective-permute-done.38.refs_1_, bf16[128,192,384]{2,1,0:T(8,128)(2,1)} %get-tuple-element.157.refs_2_, ...), custom_call_target="tpu_custom_call", output_to_operand_aliasing={{}: (10, {})} | custom-call | flops 9000000 | bytes 56623104 | tf_op jit(solution)/shard_map/mix/pallas_call | solution.py:166
  (180 shorter events, 841.6 us)
Async XLA Ops:
  52.0 489.5 %collective-permute-start.3 = (bf16[128,96,768]{2,1,0:T(8,128)(2,1)}, bf16[128,96,768]{2,1,0:T(8,128)(2,1)}, u32[]{:S(2)}, u32[]{:S(2)}) collective-permute-start(bf16[128,96,768]{2,1,0:T(8,128)(2,1)} %get-tuple-element.85.refs_1_), channel_id=1, source_target_pairs={{0,1},{1,0},{2,3},{3,2},{4,5},{5,4},{6,7},{7,6},{8,9},{9,8},{10,11... | collective-permute-start | bytes 56623112 | tf_op jit(solution)/shard_map/ppermute | solution.py:190
  100.0 444.0 %collective-permute-start.2 = (bf16[128,96,768]{2,1,0:T(8,128)(2,1)}, bf16[128,96,768]{2,1,0:T(8,128)(2,1)}, u32[]{:S(2)}, u32[]{:S(2)}) collective-permute-start(bf16[128,96,768]{2,1,0:T(8,128)(2,1)} %get-tuple-element.83.refs_1_), channel_id=1, source_target_pairs={{0,1},{1,0},{2,3},{3,2},{4,5},{5,4},{6,7},{7,6},{8,9},{9,8},{10,11... | collective-permute-start | bytes 56623112 | tf_op jit(solution)/shard_map/ppermute | solution.py:190
  100.5 525.8 %collective-permute-start = (bf16[96,768,128]{2,1,0:T(8,128)(2,1)}, bf16[96,768,128]{2,1,0:T(8,128)(2,1)}, u32[]{:S(2)}, u32[]{:S(2)}) collective-permute-start(bf16[96,768,128]{2,1,0:T(8,128)(2,1)} %refs_3_.10), channel_id=1, source_target_pairs={{2,0},{3,1},{4,2},{5,3},{6,4},{7,5},{0,6},{1,7},{10,8},{11,9},{12,... | collective-permute-start | bytes 56623112 | tf_op jit(solution)/shard_map/ppermute | solution.py:187
  104.4 521.9 %collective-permute-start.1 = (bf16[96,768,128]{2,1,0:T(8,128)(2,1)}, bf16[96,768,128]{2,1,0:T(8,128)(2,1)}, u32[]{:S(2)}, u32[]{:S(2)}) collective-permute-start(bf16[96,768,128]{2,1,0:T(8,128)(2,1)} %refs_3_.11), channel_id=1, source_target_pairs={{6,0},{7,1},{0,2},{1,3},{2,4},{3,5},{4,6},{5,7},{14,8},{15,9},{8,1... | collective-permute-start | bytes 56623112 | tf_op jit(solution)/shard_map/ppermute | solution.py:187
  104.5 413.1 %collective-permute-start.4 = (s32[96,768]{0,1:T(8,128)S(1)}, s32[96,768]{0,1:T(8,128)S(1)}, u32[]{:S(2)}, u32[]{:S(2)}) collective-permute-start(s32[96,768]{0,1:T(8,128)S(1)} %copy.16), channel_id=1, source_target_pairs={{2,0},{3,1},{4,2},{5,3},{6,4},{7,5},{0,6},{1,7},{10,8},{11,9},{12,... | collective-permute-start | bytes 884744 | tf_op jit(solution)/shard_map/ppermute | solution.py:187
  675.2 162.7 %collective-permute-start.13 = (bf16[128,96,768]{2,1,0:T(8,128)(2,1)}, bf16[128,96,768]{2,1,0:T(8,128)(2,1)}, u32[]{:S(2)}, u32[]{:S(2)}) collective-permute-start(bf16[128,96,768]{2,1,0:T(8,128)(2,1)} %get-tuple-element.95.refs_1_), channel_id=1, source_target_pairs={{0,1},{1,0},{2,3},{3,2},{4,5},{5,4},{6,7},{7,6},{8,9},{9,8},{10,11... | collective-permute-start | bytes 56623112 | tf_op jit(solution)/shard_map/ppermute | solution.py:190
  724.0 161.7 %collective-permute-start.12 = (bf16[128,96,768]{2,1,0:T(8,128)(2,1)}, bf16[128,96,768]{2,1,0:T(8,128)(2,1)}, u32[]{:S(2)}, u32[]{:S(2)}) collective-permute-start(bf16[128,96,768]{2,1,0:T(8,128)(2,1)} %get-tuple-element.94.refs_1_), channel_id=1, source_target_pairs={{0,1},{1,0},{2,3},{3,2},{4,5},{5,4},{6,7},{7,6},{8,9},{9,8},{10,11... | collective-permute-start | bytes 56623112 | tf_op jit(solution)/shard_map/ppermute | solution.py:190
  724.6 407.6 %collective-permute-start.10 = (bf16[96,768,128]{2,1,0:T(8,128)(2,1)}, bf16[96,768,128]{2,1,0:T(8,128)(2,1)}, u32[]{:S(2)}, u32[]{:S(2)}) collective-permute-start(bf16[96,768,128]{2,1,0:T(8,128)(2,1)} %collective-permute-done.refs_0_.refs_3_), channel_id=1, source_target_pairs={{2,0},{3,1},{4,2},{5,3},{6,4},{7,5},{0,6},{1,7},{10,8},{11,9},{12,... | collective-permute-start | bytes 56623112 | tf_op jit(solution)/shard_map/ppermute | solution.py:187
  726.1 408.4 %collective-permute-start.11 = (bf16[96,768,128]{2,1,0:T(8,128)(2,1)}, bf16[96,768,128]{2,1,0:T(8,128)(2,1)}, u32[]{:S(2)}, u32[]{:S(2)}) collective-permute-start(bf16[96,768,128]{2,1,0:T(8,128)(2,1)} %collective-permute-done.1.refs_0_.refs_3_), channel_id=1, source_target_pairs={{6,0},{7,1},{0,2},{1,3},{2,4},{3,5},{4,6},{5,7},{14,8},{15,9},{8,1... | collective-permute-start | bytes 56623112 | tf_op jit(solution)/shard_map/ppermute | solution.py:187
  1212.7 204.6 %collective-permute-start.18 = (bf16[192,96,128]{2,1,0:T(8,128)(2,1)}, bf16[192,96,128]{2,1,0:T(8,128)(2,1)}, u32[]{:S(2)}, u32[]{:S(2)}) collective-permute-start(bf16[192,96,128]{2,1,0:T(8,128)(2,1)} %bitcast.128), channel_id=1, source_target_pairs={{2,0},{3,1},{4,2},{5,3},{6,4},{7,5},{0,6},{1,7},{10,8},{11,9},{12,... | collective-permute-start | bytes 14155784 | tf_op jit(solution)/shard_map/ppermute | solution.py:187
  1213.8 203.5 %collective-permute-start.20 = (bf16[192,96,128]{2,1,0:T(8,128)(2,1)}, bf16[192,96,128]{2,1,0:T(8,128)(2,1)}, u32[]{:S(2)}, u32[]{:S(2)}) collective-permute-start(bf16[192,96,128]{2,1,0:T(8,128)(2,1)} %bitcast.123), channel_id=1, source_target_pairs={{6,0},{7,1},{0,2},{1,3},{2,4},{3,5},{4,6},{5,7},{14,8},{15,9},{8,1... | collective-permute-start | bytes 14155784 | tf_op jit(solution)/shard_map/ppermute | solution.py:187
  1580.8 177.0 %collective-permute-start.24 = (bf16[192,96,128]{2,1,0:T(8,128)(2,1)}, bf16[192,96,128]{2,1,0:T(8,128)(2,1)}, u32[]{:S(2)}, u32[]{:S(2)}) collective-permute-start(bf16[192,96,128]{2,1,0:T(8,128)(2,1)} %bitcast.125), channel_id=1, source_target_pairs={{2,0},{3,1},{4,2},{5,3},{6,4},{7,5},{0,6},{1,7},{10,8},{11,9},{12,... | collective-permute-start | bytes 14155784 | tf_op jit(solution)/shard_map/ppermute | solution.py:187
  1608.3 178.6 %collective-permute-start.25 = (bf16[192,96,128]{2,1,0:T(8,128)(2,1)}, bf16[192,96,128]{2,1,0:T(8,128)(2,1)}, u32[]{:S(2)}, u32[]{:S(2)}) collective-permute-start(bf16[192,96,128]{2,1,0:T(8,128)(2,1)} %collective-permute-done.18.refs_1_), channel_id=1, source_target_pairs={{2,0},{3,1},{4,2},{5,3},{6,4},{7,5},{0,6},{1,7},{10,8},{11,9},{12,... | collective-permute-start | bytes 14155784 | tf_op jit(solution)/shard_map/ppermute | solution.py:187
  1635.3 251.9 %collective-permute-start.26 = (bf16[192,96,128]{2,1,0:T(8,128)(2,1)}, bf16[192,96,128]{2,1,0:T(8,128)(2,1)}, u32[]{:S(2)}, u32[]{:S(2)}) collective-permute-start(bf16[192,96,128]{2,1,0:T(8,128)(2,1)} %collective-permute-done.19.refs_2_), channel_id=1, source_target_pairs={{2,0},{3,1},{4,2},{5,3},{6,4},{7,5},{0,6},{1,7},{10,8},{11,9},{12,... | collective-permute-start | bytes 14155784 | tf_op jit(solution)/shard_map/ppermute | solution.py:187
  1939.8 308.0 %collective-permute-start.30 = (bf16[128,192,384]{2,1,0:T(8,128)(2,1)}, bf16[128,192,384]{2,1,0:T(8,128)(2,1)}, u32[]{:S(2)}, u32[]{:S(2)}) collective-permute-start(bf16[128,192,384]{2,1,0:T(8,128)(2,1)} %project.20.refs_2_), channel_id=1, source_target_pairs={{0,1},{1,0},{2,3},{3,2},{4,5},{5,4},{6,7},{7,6},{8,9},{9,8},{10,11... | collective-permute-start | bytes 56623112 | tf_op jit(solution)/shard_map/ppermute | solution.py:190
  1939.9 207.3 %collective-permute-start.32 = (bf16[192,96,128]{2,1,0:T(8,128)(2,1)}, bf16[192,96,128]{2,1,0:T(8,128)(2,1)}, u32[]{:S(2)}, u32[]{:S(2)}) collective-permute-start(bf16[192,96,128]{2,1,0:T(8,128)(2,1)} %bitcast.116), channel_id=1, source_target_pairs={{6,0},{7,1},{0,2},{1,3},{2,4},{3,5},{4,6},{5,7},{14,8},{15,9},{8,1... | collective-permute-start | bytes 14155784 | tf_op jit(solution)/shard_map/ppermute | solution.py:187
  1940.1 307.8 %collective-permute-start.33 = (bf16[192,96,128]{2,1,0:T(8,128)(2,1)}, bf16[192,96,128]{2,1,0:T(8,128)(2,1)}, u32[]{:S(2)}, u32[]{:S(2)}) collective-permute-start(bf16[192,96,128]{2,1,0:T(8,128)(2,1)} %bitcast.120), channel_id=1, source_target_pairs={{6,0},{7,1},{0,2},{1,3},{2,4},{3,5},{4,6},{5,7},{14,8},{15,9},{8,1... | collective-permute-start | bytes 14155784 | tf_op jit(solution)/shard_map/ppermute | solution.py:187
  1942.8 344.9 %collective-permute-start.14 = (bf16[192,96,128]{2,1,0:T(8,128)(2,1)}, bf16[192,96,128]{2,1,0:T(8,128)(2,1)}, u32[]{:S(2)}, u32[]{:S(2)}) collective-permute-start(bf16[192,96,128]{2,1,0:T(8,128)(2,1)} %bitcast.121), channel_id=1, source_target_pairs={{2,0},{3,1},{4,2},{5,3},{6,4},{7,5},{0,6},{1,7},{10,8},{11,9},{12,... | collective-permute-start | bytes 14155784 | tf_op jit(solution)/shard_map/ppermute | solution.py:187
  2046.1 241.6 %collective-permute-start.17 = (bf16[192,96,128]{2,1,0:T(8,128)(2,1)}, bf16[192,96,128]{2,1,0:T(8,128)(2,1)}, u32[]{:S(2)}, u32[]{:S(2)}) collective-permute-start(bf16[192,96,128]{2,1,0:T(8,128)(2,1)} %bitcast.106.refs_0_), channel_id=1, source_target_pairs={{2,0},{3,1},{4,2},{5,3},{6,4},{7,5},{0,6},{1,7},{10,8},{11,9},{12,... | collective-permute-start | bytes 14155784 | tf_op jit(solution)/shard_map/ppermute | solution.py:187
  2289.8 204.0 %collective-permute-start.37 = (bf16[192,96,128]{2,1,0:T(8,128)(2,1)}, bf16[192,96,128]{2,1,0:T(8,128)(2,1)}, u32[]{:S(2)}, u32[]{:S(2)}) collective-permute-start(bf16[192,96,128]{2,1,0:T(8,128)(2,1)} %collective-permute-done.32.refs_2_), channel_id=1, source_target_pairs={{6,0},{7,1},{0,2},{1,3},{2,4},{3,5},{4,6},{5,7},{14,8},{15,9},{8,1... | collective-permute-start | bytes 14155784 | tf_op jit(solution)/shard_map/ppermute | solution.py:187
  2494.3 164.5 %collective-permute-start.38 = (bf16[128,192,384]{2,1,0:T(8,128)(2,1)}, bf16[128,192,384]{2,1,0:T(8,128)(2,1)}, u32[]{:S(2)}, u32[]{:S(2)}) collective-permute-start(bf16[128,192,384]{2,1,0:T(8,128)(2,1)} %get-tuple-element.150.refs_0_), channel_id=1, source_target_pairs={{0,1},{1,0},{2,3},{3,2},{4,5},{5,4},{6,7},{7,6},{8,9},{9,8},{10,11... | collective-permute-start | bytes 56623112 | tf_op jit(solution)/shard_map/ppermute | solution.py:190
  2494.3 204.4 %collective-permute-start.40 = (bf16[128,192,384]{2,1,0:T(8,128)(2,1)}, bf16[128,192,384]{2,1,0:T(8,128)(2,1)}, u32[]{:S(2)}, u32[]{:S(2)}) collective-permute-start(bf16[128,192,384]{2,1,0:T(8,128)(2,1)} %get-tuple-element.157.refs_2_), channel_id=1, source_target_pairs={{0,1},{1,0},{2,3},{3,2},{4,5},{5,4},{6,7},{7,6},{8,9},{9,8},{10,11... | collective-permute-start | bytes 56623112 | tf_op jit(solution)/shard_map/ppermute | solution.py:190
  2547.7 191.3 %collective-permute-start.39 = (bf16[128,192,384]{2,1,0:T(8,128)(2,1)}, bf16[128,192,384]{2,1,0:T(8,128)(2,1)}, u32[]{:S(2)}, u32[]{:S(2)}) collective-permute-start(bf16[128,192,384]{2,1,0:T(8,128)(2,1)} %project.23.refs_2_), channel_id=1, source_target_pairs={{0,1},{1,0},{2,3},{3,2},{4,5},{5,4},{6,7},{7,6},{8,9},{9,8},{10,11... | collective-permute-start | bytes 56623112 | tf_op jit(solution)/shard_map/ppermute | solution.py:190
  2589.2 189.7 %collective-permute-start.43 = (bf16[96,192,128]{2,1,0:T(8,128)(2,1)}, bf16[96,192,128]{2,1,0:T(8,128)(2,1)}, u32[]{:S(2)}, u32[]{:S(2)}) collective-permute-start(bf16[96,192,128]{2,1,0:T(8,128)(2,1)} %mix.28), channel_id=1, source_target_pairs={{2,0},{3,1},{4,2},{5,3},{6,4},{7,5},{0,6},{1,7},{10,8},{11,9},{12,... | collective-permute-start | bytes 14155784 | tf_op jit(solution)/shard_map/ppermute | solution.py:187
  (38 other events, 6114.8 us)
